TPU v7x, 16 devices: a whole 2x2x2 slice. The times are simulated.
16 devices in a mesh: dp: 2 (over z), tp: 8 (over y, x, core).
Axes of the slice: x: 2, y: 2, z: 2, core: 2. Of those that a mesh axis runs over, the one named last changes fastest.
Arguments:
- x_seq: bfloat16 [3, 256, 5120], P(None, 'dp'), parts along dimension 1
- cache_len: int32 [256], P('dp'), parts along dimension 0
- k_cache: bfloat16 [256, 8, 256, 128], P('dp', 'tp'), parts along dimension 0
- v_cache: bfloat16 [256, 8, 256, 128], P('dp', 'tp'), parts along dimension 0
- w_q: bfloat16 [5120, 5120], P(None, 'tp')
- w_k: bfloat16 [5120, 1024], P(None, 'tp')
- w_v: bfloat16 [5120, 1024], P(None, 'tp')
- w_o: bfloat16 [5120, 5120], P('tp')
- w_gate: bfloat16 [5120, 13824], P(None, 'tp')
- w_up: bfloat16 [5120, 13824], P(None, 'tp')
- w_down: bfloat16 [13824, 5120], P('tp')
- g_q: bfloat16 [5120], P('tp')
- g_k: bfloat16 [1024], P('tp')
- g_attn: bfloat16 [5120], replicated
- g_mlp: bfloat16 [5120], replicated
Outputs:
- output 1: bfloat16 [3, 256, 5120], P(None, 'dp'), parts along dimension 1
- output 2: bfloat16 [256, 8, 256, 128], P('dp', 'tp'), parts along dimension 0
- output 3: bfloat16 [256, 8, 256, 128], P('dp', 'tp'), parts along dimension 0
There are 2 independent parts. A program takes and returns all parts, laid end to end along the dimension named above; an argument that names none is the same for every part.
All inputs are finite; a program needn't handle non-finite values.
Results may differ from a plain program's by a relative error of at most 0.02.
Values are sent between devices in bfloat16 or wider.
A program may use at most 1 GiB of HBM per device.

v0:
```python
import jax
import jax.numpy as jnp
from jax import lax
from jax.sharding import PartitionSpec as P

ROPE_THETA = 500000.0
NORM_EPS = 1e-6


def rms_factor(sq_sum, full_width):
    return lax.rsqrt(sq_sum / full_width + NORM_EPS)


def rope_tables(positions, head_dim):
    half_dim = head_dim // 2
    inv_freq = ROPE_THETA ** (-(jnp.arange(half_dim, dtype=jnp.float32) * (2.0 / head_dim)))
    angles = positions.astype(jnp.float32)[:, None] * inv_freq[None, :]
    return jnp.cos(angles), jnp.sin(angles)


def apply_rope(head_vals, cos_tab, sin_tab):
    half_dim = head_vals.shape[-1] // 2
    lead_half = head_vals[..., :half_dim]
    tail_half = head_vals[..., half_dim:]
    cos_rows = cos_tab[:, None, :]
    sin_rows = sin_tab[:, None, :]
    return jnp.concatenate([lead_half * cos_rows - tail_half * sin_rows, tail_half * cos_rows + lead_half * sin_rows], axis=-1)


def attend(q_rot, k_old, v_old, lengths, new_keys, new_vals):
    score_scale = q_rot.shape[-1] ** -0.5
    seq_max = k_old.shape[2]
    old_scores = jnp.einsum('bkgd,bksd->bkgs', q_rot, k_old, preferred_element_type=jnp.float32) * score_scale
    old_valid = jnp.arange(seq_max)[None, :] < lengths[:, None]
    old_scores = jnp.where(old_valid[:, None, None, :], old_scores, -jnp.inf)
    new_scores = jnp.einsum('bkgd,bktd->bkgt', q_rot, new_keys, preferred_element_type=jnp.float32) * score_scale
    row_max = jnp.maximum(jnp.max(old_scores, axis=-1, keepdims=True), jnp.max(new_scores, axis=-1, keepdims=True))
    old_exp = jnp.exp(old_scores - row_max)
    new_exp = jnp.exp(new_scores - row_max)
    row_sum = jnp.sum(old_exp, axis=-1, keepdims=True) + jnp.sum(new_exp, axis=-1, keepdims=True)
    mixed_vals = jnp.einsum('bkgs,bksd->bkgd', old_exp.astype(jnp.bfloat16), v_old, preferred_element_type=jnp.float32) + jnp.einsum('bkgt,bktd->bkgd', new_exp.astype(jnp.bfloat16), new_vals, preferred_element_type=jnp.float32)
    return (mixed_vals / row_sum).astype(jnp.bfloat16)


def group_psum(part_val):
    return lax.psum(part_val, 'tp')


def layer_steps(x_seq, cache_len, k_cache, v_cache, w_q, w_k, w_v, w_o, w_gate, w_up, w_down, g_q, g_k, g_attn, g_mlp, q_width, kv_width, group_sum):
    num_steps, n_rows, d_model = x_seq.shape
    kv_loc = k_cache.shape[1]
    head_dim = k_cache.shape[-1]
    q_loc = w_q.shape[1] // head_dim
    group_size = q_loc // kv_loc
    gain_q = g_q.astype(jnp.float32)
    gain_k = g_k.astype(jnp.float32)
    gain_a = g_attn.astype(jnp.float32)
    gain_m = g_mlp.astype(jnp.float32)
    new_keys = []
    new_vals = []
    y_list = []
    for step_idx in range(num_steps):
        x_tok = x_seq[step_idx]
        positions = cache_len + step_idx
        q_raw = jnp.dot(x_tok, w_q, preferred_element_type=jnp.float32).astype(jnp.bfloat16).astype(jnp.float32)
        k_raw = jnp.dot(x_tok, w_k, preferred_element_type=jnp.float32).astype(jnp.bfloat16).astype(jnp.float32)
        v_new = jnp.dot(x_tok, w_v, preferred_element_type=jnp.float32).astype(jnp.bfloat16)
        q_sq = group_sum(jnp.sum(q_raw * q_raw, axis=-1, keepdims=True))
        k_sq = group_sum(jnp.sum(k_raw * k_raw, axis=-1, keepdims=True))
        cos_tab, sin_tab = rope_tables(positions, head_dim)
        q_normed = (q_raw * rms_factor(q_sq, q_width) * gain_q).reshape(n_rows, q_loc, head_dim)
        k_normed = (k_raw * rms_factor(k_sq, kv_width) * gain_k).reshape(n_rows, kv_loc, head_dim)
        q_rot = apply_rope(q_normed, cos_tab, sin_tab).astype(jnp.bfloat16).reshape(n_rows, kv_loc, group_size, head_dim)
        new_keys.append(apply_rope(k_normed, cos_tab, sin_tab).astype(jnp.bfloat16))
        new_vals.append(v_new.reshape(n_rows, kv_loc, head_dim))
        attn_vals = attend(q_rot, k_cache, v_cache, cache_len, jnp.stack(new_keys, axis=2), jnp.stack(new_vals, axis=2))
        attn_part = jnp.dot(attn_vals.reshape(n_rows, q_loc * head_dim), w_o, preferred_element_type=jnp.float32).astype(jnp.bfloat16)
        attn_sum = group_sum(attn_part).astype(jnp.float32)
        hidden = (x_tok.astype(jnp.float32) + attn_sum * rms_factor(jnp.sum(attn_sum * attn_sum, axis=-1, keepdims=True), d_model) * gain_a).astype(jnp.bfloat16)
        gate_pre = jnp.dot(hidden, w_gate, preferred_element_type=jnp.float32)
        up_pre = jnp.dot(hidden, w_up, preferred_element_type=jnp.float32)
        act_loc = (jax.nn.silu(gate_pre) * up_pre).astype(jnp.bfloat16)
        mlp_part = jnp.dot(act_loc, w_down, preferred_element_type=jnp.float32).astype(jnp.bfloat16)
        mlp_sum = group_sum(mlp_part).astype(jnp.float32)
        y_tok = (hidden.astype(jnp.float32) + mlp_sum * rms_factor(jnp.sum(mlp_sum * mlp_sum, axis=-1, keepdims=True), d_model) * gain_m).astype(jnp.bfloat16)
        y_list.append(y_tok)
    offsets = jnp.arange(k_cache.shape[2], dtype=jnp.int32)[None, None, :, None] - cache_len[:, None, None, None]
    k_out = k_cache
    v_out = v_cache
    for step_idx in range(num_steps):
        at_slot = offsets == step_idx
        k_out = jnp.where(at_slot, new_keys[step_idx][:, :, None, :], k_out)
        v_out = jnp.where(at_slot, new_vals[step_idx][:, :, None, :], v_out)
    return jnp.stack(y_list), k_out, v_out


def solution(mesh):
    tp_size = mesh.shape['tp']

    def local_run(x_seq, cache_len, k_cache, v_cache, w_q, w_k, w_v, w_o, w_gate, w_up, w_down, g_q, g_k, g_attn, g_mlp):
        return layer_steps(x_seq, cache_len, k_cache, v_cache, w_q, w_k, w_v, w_o, w_gate, w_up, w_down, g_q, g_k, g_attn, g_mlp, w_q.shape[1] * tp_size, w_k.shape[1] * tp_size, group_psum)

    data_spec = P(None, 'dp', None)
    cache_spec = P('dp', 'tp', None, None)
    col_spec = P(None, 'tp')
    row_spec = P('tp', None)
    arg_specs = (data_spec, P('dp'), cache_spec, cache_spec, col_spec, col_spec, col_spec, row_spec, col_spec, col_spec, row_spec, P('tp'), P('tp'), P(None), P(None))
    out_specs = (data_spec, cache_spec, cache_spec)
    return jax.shard_map(local_run, mesh=mesh, in_specs=arg_specs, out_specs=out_specs, check_vma=False)
```

profile of v0, /device:TPU:0, one launch (start us, length us, event | category | flops | bytes accessed | tf_op | source)
XLA Modules:
  0.0 339.1 jit_solution(12080315661734423719)
XLA Ops:
  7.2 1.2 copy-done
  8.5 2.6 fusion.133
  11.1 2.0 fusion.124
  13.1 0.7 multiply_reduce_fusion.5
  13.7 0.7 multiply_reduce_fusion.3
  14.4 0.7 multiply_reduce_fusion.4
  15.1 1.2 fusion.218
  16.2 0.8 fusion.166
  17.0 1.3 multiply_reduce_fusion.2
  18.3 1.3 multiply_reduce_fusion
  19.6 1.3 multiply_reduce_fusion.1
  20.9 15.6 %all-reduce = (f32[128,1]{0,1:T(1,128)S(1)}, f32[128,1]{0,1:T(1,128)S(1)}, f32[128,1]{0,1:T(1,128)S(1)}, f32[128,1]{0,1:T(1,128)S(1)}, f32[128,1]{0,1:T(1,128)S(1)}, /*index=5*/f32[128,1]{0,1:T(1,128)S(1)}) all-reduce(f32[128,1]{0,1:T(1,128)S(1)} %bitcast.243, f32[128,1]{0,1:T(1,128)S(1)} %bitcast.240, ...), channel_id=1, replica_groups=mesh['dp'=2,'tp'=8] {'tp'}, use_global_device_ids=true, to_apply=%region_23.24 | all-reduce | flops 768 | bytes 6144 | tf_op jit(solution)/shard_map/psum | solution.py:46
  36.6 1.0 multiply_cosine_fusion.2
  40.8 5.9 %fusion.213 = (f32[128,5]{1,0:T(8,128)S(1)}, f32[128,5,256]{2,1,0:T(8,128)S(1)}) fusion(bf16[128,1,256,128]{3,2,1,0:T(8,128)(2,1)} %param.17, bf16[128,5,64]{2,1,0:T(8,128)(2,1)S(1)} %get-tuple-element.23, bf16[128,5,64]{2,1,0:T(8,128)(2,1)S(1)} %get-tuple-element.22, pred[128,256]{1,0:T(8,128)(4,1)S(1)} %get-tuple-element.57), kind=kOutput, calls=%fused_computation.253 | convolution fusion | flops 42761600 | bytes 9243136 | tf_op jit(solution)/shard_map/bkgd,bksd->bkgs/dot_general | solution.py:33
  46.9 5.9 %fusion.215 = (f32[128,5]{1,0:T(8,128)S(1)}, f32[128,5,256]{2,1,0:T(8,128)S(1)}) fusion(bf16[128,1,256,128]{3,2,1,0:T(8,128)(2,1)} %param.17, bf16[128,5,64]{2,1,0:T(8,128)(2,1)S(1)} %get-tuple-element.21, bf16[128,5,64]{2,1,0:T(8,128)(2,1)S(1)} %get-tuple-element.20, pred[128,256]{1,0:T(8,128)(4,1)S(1)} %get-tuple-element.57), kind=kOutput, calls=%fused_computation.255 | convolution fusion | flops 42761600 | bytes 9243136 | tf_op jit(solution)/shard_map/bkgd,bksd->bkgs/dot_general | solution.py:33
  52.8 1.1 fusion.216
  54.3 1.2 fusion.2
  56.0 1.2 fusion
  57.3 0.6 maximum_bitcast_fusion.3
  57.9 0.7 maximum_bitcast_fusion.1
  59.6 5.8 %fusion.217 = (f32[128,5]{1,0:T(8,128)S(1)}, f32[128,5,256]{2,1,0:T(8,128)S(1)}) fusion(bf16[128,1,256,128]{3,2,1,0:T(8,128)(2,1)} %param.17, bf16[128,5,64]{2,1,0:T(8,128)(2,1)S(1)} %get-tuple-element.19, bf16[128,5,64]{2,1,0:T(8,128)(2,1)S(1)} %get-tuple-element.18, pred[128,256]{1,0:T(8,128)(4,1)S(1)} %get-tuple-element.57), kind=kOutput, calls=%fused_computation.257 | convolution fusion | flops 42761600 | bytes 9243136 | tf_op jit(solution)/shard_map/bkgd,bksd->bkgs/dot_general | solution.py:33
  66.3 5.1 %fusion.86 = bf16[128,5,128]{2,1,0:T(8,128)(2,1)S(1)} fusion(bf16[128,1,256,128]{3,2,1,0:T(8,128)(2,1)} %param.18, f32[128,5,256]{2,1,0:T(8,128)S(1)} %get-tuple-element.93, f32[128,5]{1,0:T(8,128)S(1)} %multiply_maximum_fusion, f32[128,5]{1,0:T(8,128)S(1)} %get-tuple-element.31, f32[128,128]{1,0:T(8,128)S(1)} %copy-done.39, f32[128,5]{1,0:T(8,128)S(1)} %get-tuple-element.30), kind=kOutput, calls=%fused_computation.96 | convolution fusion | flops 42598400 | bytes 9281024 | tf_op jit(solution)/shard_map/bkgs,bksd->bkgd/dot_general | solution.py:41
  73.3 5.3 %convolution_convert_fusion.1 = bf16[128,5120]{1,0:T(8,128)(2,1)} fusion(bf16[128,640]{0,1:T(8,128)(2,1)S(1)} %bitcast.215, bf16[640,5120]{1,0:T(8,128)(2,1)} %param.22), kind=kOutput, calls=%fused_computation.15 | convolution fusion | flops 839516160 | bytes 8028160 | tf_op jit(solution)/shard_map/dot_general | solution.py:77
  78.6 5.3 %convolution_convert_fusion.3 = bf16[128,5120]{1,0:T(8,128)(2,1)} fusion(bf16[128,640]{0,1:T(8,128)(2,1)S(1)} %bitcast.214, bf16[640,5120]{1,0:T(8,128)(2,1)} %param.22), kind=kOutput, calls=%fused_computation.17 | convolution fusion | flops 839516160 | bytes 8028160 | tf_op jit(solution)/shard_map/dot_general | solution.py:77
  83.9 2.3 convolution_convert_fusion.5
  86.9 0.6 convert_element_type.249
  87.6 0.7 copy.42
  88.3 0.7 copy.41
  89.0 0.7 copy.43
  89.7 66.0 %all-reduce.8.cloned.1.call-done = (bf16[128,5120]{1,0:T(8,128)(2,1)}, bf16[128,5120]{1,0:T(8,128)(2,1)}, bf16[128,5120]{1,0:T(8,128)(2,1)}) async-done(((bf16[128,5120]{1,0:T(8,128)(2,1)}, bf16[128,5120]{1,0:T(8,128)(2,1)}, bf16[128,5120]{1,0:T(8,128)(2,1)}), (bf16[128,5120]{1,0:T(8,128)(2,1)}, bf16[128,5120]{1,0:T(8,128)(2,1)}, bf16[128,5120]{1,0:T(8,128)(2,1)})) %all-reduce.8.cloned.1.call-update) | async-done | bytes 3932176 | tf_op jit(solution)/shard_map/psum | solution.py:46
  155.8 1.8 fusion.28
  157.6 1.7 fusion.20
  159.3 1.7 fusion.12
  161.0 4.2 %fusion.15 = (bf16[128,5120]{1,0:T(8,128)(2,1)S(1)}, bf16[128,5120]{1,0:T(8,128)(2,1)S(1)}, bf16[128,5120]{1,0:T(8,128)(2,1)}) fusion(bf16[128,5120]{1,0:T(8,128)(2,1)} %get-tuple-element.14, f32[5120]{0:T(1024)S(1)} %convert_element_type.243, f32[128]{0:T(128)S(1)} %add_rsqrt_fusion.5, bf16[3,128,5120]{2,1,0:T(8,128)(2,1)S(1)} %copy-done.3, ...), kind=kLoop, calls=%fused_computation.36 | loop fusion | flops 11796480 | bytes 11818496 | tf_op jit(solution)/shard_map/convert_element_type | solution.py:79
  165.2 9.6 %fusion.219 = f32[128,1728]{0,1:T(8,128)} fusion(bf16[128,5120]{1,0:T(8,128)(2,1)S(1)} %get-tuple-element.15, bf16[5120,1728]{0,1:T(8,128)(2,1)} %param.23), kind=kOutput, calls=%fused_computation.259 | convolution fusion | flops 2264924160 | bytes 19890176 | tf_op jit(solution)/shard_map/dot_general | solution.py:80
  174.8 4.8 %fusion.220 = f32[128,1728]{0,1:T(8,128)S(1)} fusion(bf16[128,5120]{1,0:T(8,128)(2,1)S(1)} %get-tuple-element.16, bf16[5120,1728]{0,1:T(8,128)(2,1)S(1)} %bitcast.203), kind=kOutput, calls=%fused_computation.260 | convolution fusion | flops 2264924160 | bytes 19890176 | tf_op jit(solution)/shard_map/dot_general | solution.py:80
  179.6 20.8 %convolution_convert_fusion.4 = bf16[128,5120]{1,0:T(8,128)(2,1)} fusion(bf16[1728,5120]{1,0:T(8,128)(2,1)} %param.25, bf16[128,5120]{1,0:T(8,128)(2,1)S(1)} %get-tuple-element.15, bf16[5120,1728]{0,1:T(8,128)(2,1)} %param.24, f32[128,1728]{0,1:T(8,128)} %fusion.219), kind=kOutput, calls=%fused_computation.18 | convolution fusion | flops 4531830784 | bytes 38895616 | tf_op jit(solution)/shard_map/dot_general | solution.py:83
  200.4 20.5 %convolution_convert_fusion.2 = bf16[128,5120]{1,0:T(8,128)(2,1)} fusion(bf16[1728,5120]{1,0:T(8,128)(2,1)} %param.25, bf16[128,5120]{1,0:T(8,128)(2,1)S(1)} %get-tuple-element.16, bf16[5120,1728]{0,1:T(8,128)(2,1)} %param.24, f32[128,1728]{0,1:T(8,128)S(1)} %fusion.220), kind=kOutput, calls=%fused_computation.16 | convolution fusion | flops 4531830784 | bytes 38895616 | tf_op jit(solution)/shard_map/dot_general | solution.py:83
  220.9 9.1 %fusion.221 = f32[128,1728]{0,1:T(8,128)S(1)} fusion(bf16[128,5120]{1,0:T(8,128)(2,1)} %get-tuple-element.17, bf16[5120,1728]{0,1:T(8,128)(2,1)} %param.23), kind=kOutput, calls=%fused_computation.261 | convolution fusion | flops 2264924160 | bytes 19890176 | tf_op jit(solution)/shard_map/dot_general | solution.py:80
  230.0 21.0 %convolution_convert_fusion = bf16[128,5120]{1,0:T(8,128)(2,1)} fusion(bf16[1728,5120]{1,0:T(8,128)(2,1)} %param.25, bf16[128,5120]{1,0:T(8,128)(2,1)} %get-tuple-element.17, bf16[5120,1728]{0,1:T(8,128)(2,1)} %param.24, f32[128,1728]{0,1:T(8,128)S(1)} %fusion.221), kind=kOutput, calls=%fused_computation.14 | convolution fusion | flops 4531830784 | bytes 38895616 | tf_op jit(solution)/shard_map/dot_general | solution.py:83
  251.1 0.7 copy-done.9
  251.9 17.9 %select_select_fusion = (bf16[128,1,256,128]{3,2,1,0:T(8,128)(2,1)}, bf16[128,1,256,128]{3,2,1,0:T(8,128)(2,1)}) fusion(bf16[128,1,256,128]{3,2,1,0:T(8,128)(2,1)} %param.18, pred[128,256]{1,0:T(8,128)(4,1)S(1)} %copy-done.28, pred[128,256]{1,0:T(8,128)(4,1)S(1)} %copy-done.29, pred[128,256]{1,0:T(8,128)(4,1)S(1)} %copy-done.27, ...), kind=kLoop, calls=%fused_computation.12 | loop fusion | flops 25165824 | bytes 33849344 | tf_op jit(solution)/shard_map/jit(_where)/select_n | solution.py:93
  269.8 51.6 %all-reduce.6.cloned.1.call-done = (bf16[128,5120]{1,0:T(8,128)(2,1)}, bf16[128,5120]{1,0:T(8,128)(2,1)}, bf16[128,5120]{1,0:T(8,128)(2,1)}) async-done(((bf16[128,5120]{1,0:T(8,128)(2,1)}, bf16[128,5120]{1,0:T(8,128)(2,1)}, bf16[128,5120]{1,0:T(8,128)(2,1)}), (bf16[128,5120]{1,0:T(8,128)(2,1)}, bf16[128,5120]{1,0:T(8,128)(2,1)}, bf16[128,5120]{1,0:T(8,128)(2,1)})) %all-reduce.6.cloned.1.call-update) | async-done | bytes 3932176 | tf_op jit(solution)/shard_map/psum | solution.py:46
  321.4 1.8 fusion.32
  323.2 1.7 fusion.24
  324.9 1.7 fusion.16
  326.6 3.3 fusion.41
  329.9 2.2 pad_maximum_fusion
  (166 shorter events, 8.8 us)
Async XLA Ops:
  7.2 1.3 copy-start
  7.2 148.6 %all-reduce.8.cloned.1.call-start = ((), (), s32[]{:S(2)}) async-start(), calls=%async_computation.1 | async-start | bytes 7864320 | tf_op jit(solution)/shard_map/psum | solution.py:46
  8.5 4.5 %copy-start.2 = (bf16[3,128,5120]{2,1,0:T(8,128)(2,1)S(1)}, bf16[3,128,5120]{2,1,0:T(8,128)(2,1)}, u32[]{:S(2)}) copy-start(bf16[3,128,5120]{2,1,0:T(8,128)(2,1)} %param.15) | copy-start | bytes 11796484
  8.5 4.6 %copy-start.5 = (bf16[5120,128]{1,0:T(8,128)(2,1)S(1)}, bf16[5120,128]{1,0:T(8,128)(2,1)}, u32[]{:S(2)}) copy-start(bf16[5120,128]{1,0:T(8,128)(2,1)} %param.20) | copy-start | bytes 3932164
  11.1 6.0 %slice-start.9 = ((s8[6553600]{0:T(1024)(128)(4,1)}), s8[4194304]{0:T(1024)(128)(4,1)S(1)}, s32[]{:S(2)}) async-start(s8[6553600]{0:T(1024)(128)(4,1)} %bitcast.208), calls=%async_computation.11 | async-start | bytes 8388608
  13.7 3.3 slice-start.10
  14.4 1.8 copy-start.36
  19.6 1.3 copy-start.38
  19.6 1.3 copy-start.37
  38.1 1.1 copy-start.18
  38.1 1.1 copy-start.20
  40.8 13.5 %slice-start.7 = ((s8[8388608]{0:T(1024)(128)(4,1)}), s8[4194304]{0:T(1024)(128)(4,1)S(1)}, s32[]{:S(2)}) async-start(s8[8388608]{0:T(1024)(128)(4,1)} %bitcast.206), calls=%async_computation.9 | async-start | bytes 8388608
  46.9 7.4 %slice-start.8 = ((s8[8388608]{0:T(1024)(128)(4,1)}), s8[4194304]{0:T(1024)(128)(4,1)S(1)}, s32[]{:S(2)}) async-start(s8[8388608]{0:T(1024)(128)(4,1)} %bitcast.206), calls=%async_computation.10 | async-start | bytes 8388608
  56.0 1.3 copy-start.8
  56.0 1.9 copy-start.25
  56.0 2.8 copy-start.13
  56.0 2.8 copy-start.15
  57.3 2.2 copy-start.16
  57.3 2.2 copy-start.17
  59.6 6.6 %copy-start.39 = (f32[128,128]{1,0:T(8,128)S(1)}, f32[128,128]{1,0:T(8,128)}, u32[]{:S(2)}) copy-start(f32[128,128]{1,0:T(8,128)} %get-tuple-element.94) | copy-start | bytes 196612
  66.2 5.4 %copy-start.30 = (f32[128,5,2]{1,2,0:T(2,128)S(1)}, f32[128,5,2]{1,2,0:T(2,128)}, u32[]{:S(2)}) copy-start(f32[128,5,2]{1,2,0:T(2,128)} %get-tuple-element.91) | copy-start | bytes 15364
  66.3 5.6 %copy-start.33 = (bf16[128,2,128]{2,0,1:T(8,128)(2,1)S(1)}, bf16[128,2,128]{2,0,1:T(8,128)(2,1)}, u32[]{:S(2)}) copy-start(bf16[128,2,128]{2,0,1:T(8,128)(2,1)} %maximum_bitcast_fusion.3) | copy-start | bytes 196612
  71.4 1.3 copy-start.31
  73.3 10.6 %slice-start.5 = ((s8[6553600]{0:T(1024)(128)(4,1)}), s8[4194304]{0:T(1024)(128)(4,1)S(1)}, s32[]{:S(2)}) async-start(s8[6553600]{0:T(1024)(128)(4,1)} %bitcast.204), calls=%async_computation.7 | async-start | bytes 8388608
  78.6 5.3 %slice-start.6 = ((s8[6553600]{0:T(1024)(128)(4,1)}), s8[2359296]{0:T(1024)(128)(4,1)S(1)}, s32[]{:S(2)}) async-start(s8[6553600]{0:T(1024)(128)(4,1)} %bitcast.204), calls=%async_computation.8 | async-start | bytes 4718592
  86.2 1.3 copy-start.11
  86.2 2.1 copy-start.19
  86.2 2.1 copy-start.21
  86.3 235.2 %all-reduce.6.cloned.1.call-start = ((), (), s32[]{:S(2)}) async-start(), calls=%async_computation | async-start | bytes 7864320 | tf_op jit(solution)/shard_map/psum | solution.py:46
  155.8 5.2 %copy-start.3 = (bf16[3,128,5120]{2,1,0:T(8,128)(2,1)S(1)}, bf16[3,128,5120]{2,1,0:T(8,128)(2,1)}, u32[]{:S(2)}) copy-start(bf16[3,128,5120]{2,1,0:T(8,128)(2,1)} %param.15) | copy-start | bytes 11796484
  160.9 13.8 %slice-start = ((s8[17694720]{0:T(1024)(128)(4,1)}), s8[4194304]{0:T(1024)(128)(4,1)S(1)}, s32[]{:S(2)}) async-start(s8[17694720]{0:T(1024)(128)(4,1)} %bitcast.202), calls=%async_computation.2 | async-start | bytes 8388608
  160.9 13.8 %slice-start.1 = ((s8[17694720]{0:T(1024)(128)(4,1)}), s8[4194304]{0:T(1024)(128)(4,1)S(1)}, s32[]{:S(2)}) async-start(s8[17694720]{0:T(1024)(128)(4,1)} %bitcast.202), calls=%async_computation.3 | async-start | bytes 8388608
  165.2 9.6 %slice-start.2 = ((s8[17694720]{0:T(1024)(128)(4,1)}), s8[4194304]{0:T(1024)(128)(4,1)S(1)}, s32[]{:S(2)}) async-start(s8[17694720]{0:T(1024)(128)(4,1)} %bitcast.202), calls=%async_computation.4 | async-start | bytes 8388608
  165.2 9.6 %slice-start.3 = ((s8[17694720]{0:T(1024)(128)(4,1)}), s8[4194304]{0:T(1024)(128)(4,1)S(1)}, s32[]{:S(2)}) async-start(s8[17694720]{0:T(1024)(128)(4,1)} %bitcast.202), calls=%async_computation.5 | async-start | bytes 8388608
  165.2 9.6 %slice-start.4 = ((s8[17694720]{0:T(1024)(128)(4,1)}), s8[917504]{0:T(1024)(128)(4,1)S(1)}, s32[]{:S(2)}) async-start(s8[17694720]{0:T(1024)(128)(4,1)} %bitcast.202), calls=%async_computation.6 | async-start | bytes 1835008
  251.0 0.8 copy-start.9
  251.0 0.8 copy-start.22
  251.0 0.8 copy-start.23
  251.0 0.8 copy-start.24
  251.0 0.8 copy-start.26
  251.0 0.8 copy-start.27
  251.0 0.8 copy-start.28
  251.0 0.8 copy-start.29
  251.9 74.7 %copy-start.32 = (f32[5120]{0:T(1024)S(1)}, f32[5120]{0:T(1024)}, u32[]{:S(2)}) copy-start(f32[5120]{0:T(1024)} %convert_element_type.249) | copy-start | bytes 61444
  321.4 5.2 %copy-start.4 = (bf16[128,5120]{1,0:T(8,128)(2,1)S(1)}, bf16[128,5120]{1,0:T(8,128)(2,1)}, u32[]{:S(2)}) copy-start(bf16[128,5120]{1,0:T(8,128)(2,1)} %get-tuple-element.17) | copy-start | bytes 3932164
  321.4 5.2 %copy-start.6 = (bf16[128,5120]{1,0:T(8,128)(2,1)S(1)}, bf16[128,5120]{1,0:T(8,128)(2,1)}, u32[]{:S(2)}) copy-start(bf16[128,5120]{1,0:T(8,128)(2,1)} %get-tuple-element.9) | copy-start | bytes 3932164
  321.4 5.2 %copy-start.7 = (bf16[128,5120]{1,0:T(8,128)(2,1)S(1)}, bf16[128,5120]{1,0:T(8,128)(2,1)}, u32[]{:S(2)}) copy-start(bf16[128,5120]{1,0:T(8,128)(2,1)} %get-tuple-element.10) | copy-start | bytes 3932164
  329.9 2.2 copy-start.1
  (5 other events, 3.2 us)
Sparse Core Ops, SparseCore 0:
  86.4 69.3 all-reduce.7
  251.2 70.2 all-reduce.5
where the time goes:
time: 345 us; the launch traced here: 339 us
  matrix products  138 us (40%)
  waiting for transfers between devices  118 us (34%)
  other arithmetic  44.4 us (13%)
  blocking collectives  15.6 us (5%)
  between operations  15.1 us (4%)
  local copies, waits for them, and re-layouts  8.27 us (2%)
    psum x2, waiting for transfers between devices, group_psum(): return lax.psum(part_val, 'tp')  118 us
    dot_general x3, matrix products, layer_steps(): jnp.dot(act_loc, w_down, preferred_element_type=jnp.float32)  62.3 us
    dot_general x3, matrix products, layer_steps(): gate_pre = jnp.dot(hidden, w_gate, preferred_element_type=jnp.float32)  23.4 us
    select_n x1, other arithmetic, layer_steps(): v_out = jnp.where(at_slot, new_vals[step_idx][:, :, None, :], v_out)  17.9 us
    dot_general x3, matrix products, attend(): jnp.einsum('bkgd,bksd->bkgs', q_rot, k_old, preferred_element_type=jnp.fl...  17.6 us
    psum x1, blocking collectives, group_psum(): return lax.psum(part_val, 'tp')  15.6 us
    dot_general x3, matrix products, layer_steps(): jnp.dot(attn_vals.reshape(n_rows, q_loc * head_dim), w_o, preferred_eleme...  12.9 us
    dot_general x3, matrix products, attend(): jnp.einsum('bkgs,bksd->bkgd', old_exp.astype(jnp.bfloat16), v_old, prefer...  7.6 us
  transfers between devices with their start and end apart: 2, of which 2 were waited for; matrix products, arithmetic and copies ran while one was open for 6% of the time, Pallas kernels for 0%

commit v1 on v0

v1 whole, which is shorter than its diff:
```python
import functools

import jax
import jax.numpy as jnp
from jax import lax
from jax.experimental import pallas as pl
from jax.experimental.pallas import tpu as pltpu
from jax.sharding import PartitionSpec as P

ROPE_THETA = 500000.0
NORM_EPS = 1e-6
F32 = jnp.float32
BF16 = jnp.bfloat16


def rms_factor(sq_sum, full_width):
    return lax.rsqrt(sq_sum / full_width + NORM_EPS)


def tail_kernel(dims, o_ref, ga_ref, gm_ref, x_hbm, wo_hbm, w1_hbm, w3_hbm, w2_hbm, y_hbm,
                buf, r0, r1, r2, st, own, act, w1, w3, w2, send_sem, recv_sem, w_sem, o_sem, x_sem, y_sem, free_sem):
    n_chunks, rows, d_model, q_loc, ff_loc = dims
    blk = rows // 8
    half_d = d_model // 2
    tp = lax.axis_index('tp')
    core = lax.rem(tp, 2)
    xb = lax.rem(lax.div(tp, 2), 2)
    yb = lax.div(tp, 4)
    sib = tp + 1 - 2 * core
    x_nb = tp + 2 - 4 * xb
    y_nb = tp + 4 - 8 * yb
    oc, ox, oy = 1 - core, 1 - xb, 1 - yb
    cols_a = pl.ds(0, half_d)
    cols_b = pl.ds(half_d, half_d)

    def block(c_bit, x_bit, y_bit):
        return c_bit * 4 + x_bit * 2 + y_bit

    me = block(core, xb, yb)

    wo_tile = 1024
    n_wo = d_model // wo_tile

    def wo_copy(j):
        cs = pl.ds(j * wo_tile, wo_tile)
        return pltpu.make_async_copy(wo_hbm.at[:, cs], w2.at[pl.ds(0, q_loc), cs], o_sem.at[j])

    def x_copy():
        return pltpu.make_async_copy(x_hbm.at[:, me], own, x_sem)

    n_k = 4
    k_rows = d_model // n_k

    def w13_copy(i, j):
        src, dst = ((w1_hbm, w1), (w3_hbm, w3))[i]
        rs = pl.ds(j * k_rows, k_rows)
        return pltpu.make_async_copy(src.at[rs], dst.at[rs], w_sem.at[i * n_k + j])

    f_rows = ff_loc // 4

    def w2_copy(j):
        rs = pl.ds(j * f_rows, f_rows)
        return pltpu.make_async_copy(w2_hbm.at[rs], w2.at[rs], w_sem.at[2 * n_k + j])

    for j in range(n_wo):
        wo_copy(j).start()
    x_copy().start()
    for j in range(n_k):
        for i in range(2):
            w13_copy(i, j).start()

    barrier = pltpu.get_barrier_semaphore()
    for peer in (sib, x_nb, y_nb):
        pl.semaphore_signal(barrier, inc=1, device_id={'tp': peer}, device_id_type=pl.DeviceIdType.MESH)
    pl.semaphore_wait(barrier, 3)

    def rcopy(k, c, s, src, dst, peer):
        return pltpu.make_async_remote_copy(
            src_ref=src, dst_ref=dst, send_sem=send_sem.at[k, c, s], recv_sem=recv_sem.at[k, c, s],
            device_id={'tp': peer}, device_id_type=pl.DeviceIdType.MESH)

    def xfer(k, c, s):
        b = buf.at[c]
        if s == 0:
            return rcopy(k, c, s, b.at[pl.ds(oc * 4, 4)], r0.at[c], sib)
        if s == 1:
            return rcopy(k, c, s, b.at[pl.ds(block(core, ox, 0), 2), :, cols_a], r1.at[c, :, :, cols_a], x_nb)
        if s in (2, 3):
            xx = s - 2
            return rcopy(k, c, s, b.at[block(core, xx, oy), :, cols_b], r1.at[c, xx, :, cols_b], y_nb)
        if s == 4:
            return rcopy(k, c, s, st.at[c, :, cols_a], r2.at[c, :, cols_a], y_nb)
        if s == 5:
            return rcopy(k, c, s, st.at[c, :, cols_b], r2.at[c, :, cols_b], x_nb)
        if s == 6:
            return rcopy(k, c, s, b.at[me, :, cols_a], b.at[me, :, cols_a], y_nb)
        if s == 7:
            return rcopy(k, c, s, b.at[me, :, cols_b], b.at[me, :, cols_b], x_nb)
        if s == 8:
            part = b.at[pl.ds(block(core, xb, 0), 2), :, cols_a]
            return rcopy(k, c, s, part, part, x_nb)
        if s in (9, 10):
            part = b.at[block(core, s - 9, yb), :, cols_b]
            return rcopy(k, c, s, part, part, y_nb)
        part = b.at[pl.ds(core * 4, 4)]
        return rcopy(k, c, s, part, part, sib)

    def start(k, c, *stages):
        for s in stages:
            xfer(k, c, s).start()

    def wait_recv(k, c, *stages):
        for s in stages:
            xfer(k, c, s).wait_recv()

    def wait_send(k, c, *stages):
        for s in stages:
            xfer(k, c, s).wait_send()

    v_tile = 512

    def add_cols(lo, hi, fn):
        def body(j, carry):
            fn(pl.ds(pl.multiple_of(j * v_tile, v_tile), v_tile))
            return carry
        lax.fori_loop(lo // v_tile, hi // v_tile, body, 0)

    def s0(k, c):
        start(k, c, 0)

    def s1(k, c):
        wait_recv(k, c, 0)
        wait_send(k, c, 0)
        pl.semaphore_signal(free_sem.at[k, c], inc=1, device_id={'tp': sib}, device_id_type=pl.DeviceIdType.MESH)
        mine = pl.ds(core * 4, 4)

        def add(cs):
            buf[c, mine, :, cs] = (buf[c, mine, :, cs].astype(F32) + r0[c, :, :, cs].astype(F32)).astype(BF16)
        add_cols(0, d_model, add)
        start(k, c, 1, 2, 3)

    def s2(k, c):
        wait_recv(k, c, 1, 2, 3)
        wait_send(k, c, 1, 2, 3)

        def pair(kept, sent, j_kept, j_sent, cs):
            st[c, :, cs] = (buf[c, sent, :, cs].astype(F32) + r1[c, j_sent, :, cs].astype(F32)).astype(BF16)
            buf[c, kept, :, cs] = (buf[c, kept, :, cs].astype(F32) + r1[c, j_kept, :, cs].astype(F32)).astype(BF16)

        def add_a(cs):
            pair(me, block(core, xb, oy), yb, oy, cs)

        def add_b(cs):
            pair(me, block(core, ox, yb), xb, ox, cs)
        add_cols(0, half_d, add_a)
        add_cols(half_d, d_model, add_b)
        start(k, c, 4, 5)

    def s3(k, c):
        wait_recv(k, c, 4, 5)
        wait_send(k, c, 4, 5)
        gain = ga_ref if k == 0 else gm_ref

        def total(j):
            cs = pl.ds(pl.multiple_of(j * v_tile, v_tile), v_tile)
            tot = (buf[c, me, :, cs].astype(F32) + r2[c, :, cs].astype(F32)).astype(BF16)
            buf[c, me, :, cs] = tot
            return tot.astype(F32)

        def sq_body(j, acc):
            tot = total(j)
            return acc + jnp.sum(tot * tot, axis=-1, keepdims=True)
        sq = lax.fori_loop(0, d_model // v_tile, sq_body, jnp.zeros((blk, 1), F32))
        scale = rms_factor(sq, d_model)

        def out_body(cs):
            res = (own[c, :, cs].astype(F32) + buf[c, me, :, cs].astype(F32) * scale * gain[:, cs].astype(F32)).astype(BF16)
            buf[c, me, :, cs] = res
            if k == 0:
                own[c, :, cs] = res
        add_cols(0, d_model, out_body)
        start(k, c, 6, 7)

    def g2(k, c):
        wait_recv(k, c, 6, 7)
        start(k, c, 8, 9, 10)

    def g3(k, c):
        wait_recv(k, c, 8, 9, 10)
        pl.semaphore_wait(free_sem.at[k, c], 1)
        start(k, c, 11)

    def done(k, c):
        wait_recv(k, c, 11)
        wait_send(k, c, 6, 7, 8, 9, 10, 11)

    def y_copy(c):
        return pltpu.make_async_copy(buf.at[c], y_hbm.at[c], y_sem.at[c])

    def fin(k, c):
        done(k, c)
        y_copy(c).start()

    def p1(c):
        def body(j, carry):
            cs = pl.ds(pl.multiple_of(j * wo_tile, wo_tile), wo_tile)
            acc = jnp.dot(o_ref[c], w2[0:q_loc, cs], preferred_element_type=F32)
            buf[c, :, :, cs] = acc.astype(BF16).reshape(8, blk, wo_tile)
            return carry
        lax.fori_loop(0, n_wo, body, 0)

    gu_tile = 256
    n_gu = ff_loc // gu_tile
    gu_tail = ff_loc - n_gu * gu_tile
    dn_tile = 512
    n_dn = d_model // dn_tile

    def gate_up(c, cs, width):
        h = buf[c].reshape(rows, d_model)
        gate = jnp.dot(h, w1[:, cs], preferred_element_type=F32)
        up = jnp.dot(h, w3[:, cs], preferred_element_type=F32)
        act[:, cs] = (gate * jax.nn.sigmoid(gate) * up).astype(BF16)

    def p2(services):
        n_steps = n_gu + 1 + n_dn

        def chunk(c, carry):
            def serve(step):
                for (sc, ss), fns in services.items():
                    @pl.when(jnp.logical_and(c == sc, step == ss))
                    def _(fns=fns):
                        for fn in fns:
                            fn()

            def gu_body(j, carry):
                serve(j)
                gate_up(c, pl.ds(pl.multiple_of(j * gu_tile, gu_tile), gu_tile), gu_tile)
                return carry
            lax.fori_loop(0, n_gu, gu_body, 0)
            if gu_tail:
                gate_up(c, slice(n_gu * gu_tile, ff_loc), gu_tail)

            def dn_body(j, carry):
                serve(j + n_gu)
                cs = pl.ds(pl.multiple_of(j * dn_tile, dn_tile), dn_tile)
                acc = jnp.dot(act[...], w2[:, cs], preferred_element_type=F32)
                buf[c, :, :, cs] = acc.astype(BF16).reshape(8, blk, dn_tile)
                return carry
            lax.fori_loop(0, n_dn, dn_body, 0)
            for sc in range(n_chunks):
                @pl.when(c == sc)
                def _(sc=sc):
                    s0(1, sc)
            return carry
        lax.fori_loop(0, n_chunks, chunk, 0)

    for j in range(n_wo):
        wo_copy(j).wait()
    p1(0)
    s0(0, 0)
    p1(1)
    s0(0, 1)
    s1(0, 0)
    p1(2)
    s0(0, 2)
    for j in range(4):
        w2_copy(j).start()
    s1(0, 1)
    s2(0, 0)
    s1(0, 2)
    x_copy().wait()
    s2(0, 1)
    s3(0, 0)
    s2(0, 2)
    s3(0, 1)
    g2(0, 0)
    s3(0, 2)
    g2(0, 1)
    g3(0, 0)
    for j in range(n_k):
        for i in range(2):
            w13_copy(i, j).wait()
    for j in range(4):
        w2_copy(j).wait()
    done(0, 0)

    F = functools.partial
    p2({
        (0, 0): [F(g2, 0, 2), F(g3, 0, 1)],
        (0, 4): [F(g3, 0, 2)],
        (1, 0): [F(done, 0, 1)],
        (1, 1): [F(s1, 1, 0)],
        (1, 3): [F(s2, 1, 0)],
        (1, 6): [F(s3, 1, 0)],
        (1, 10): [F(g2, 1, 0)],
        (1, 13): [F(g3, 1, 0)],
        (2, 0): [F(done, 0, 2)],
        (2, 1): [F(s1, 1, 1)],
        (2, 3): [F(s2, 1, 1)],
        (2, 6): [F(s3, 1, 1)],
        (2, 8): [F(fin, 1, 0)],
        (2, 10): [F(g2, 1, 1)],
        (2, 13): [F(g3, 1, 1)],
    })
    s1(1, 2)
    s2(1, 2)
    s3(1, 2)
    fin(1, 1)
    g2(1, 2)
    g3(1, 2)
    fin(1, 2)
    for c in range(n_chunks):
        y_copy(c).wait()


def tail(o, x_seq, w_o, w1, w3, w2, g_attn, g_mlp):
    n_chunks, rows, d_model = x_seq.shape
    q_loc = o.shape[-1]
    ff_loc = w1.shape[1]
    blk = rows // 8
    dims = (n_chunks, rows, d_model, q_loc, ff_loc)
    vmem = pl.BlockSpec(memory_space=pltpu.VMEM)
    hbm = pl.BlockSpec(memory_space=pl.ANY)
    y = pl.pallas_call(
        functools.partial(tail_kernel, dims),
        name='tail',
        out_shape=jax.ShapeDtypeStruct((n_chunks, 8, blk, d_model), BF16),
        in_specs=[vmem, vmem, vmem, hbm, hbm, hbm, hbm, hbm],
        out_specs=hbm,
        scratch_shapes=[
            pltpu.VMEM((n_chunks, 8, blk, d_model), BF16),
            pltpu.VMEM((n_chunks, 4, blk, d_model), BF16),
            pltpu.VMEM((n_chunks, 2, blk, d_model), BF16),
            pltpu.VMEM((n_chunks, blk, d_model), BF16),
            pltpu.VMEM((n_chunks, blk, d_model), BF16),
            pltpu.VMEM((n_chunks, blk, d_model), BF16),
            pltpu.VMEM((rows, ff_loc), BF16),
            pltpu.VMEM((d_model, ff_loc), BF16),
            pltpu.VMEM((d_model, ff_loc), BF16),
            pltpu.VMEM((ff_loc, d_model), BF16),
            pltpu.SemaphoreType.DMA((2, n_chunks, 12)),
            pltpu.SemaphoreType.DMA((2, n_chunks, 12)),
            pltpu.SemaphoreType.DMA((12,)),
            pltpu.SemaphoreType.DMA((d_model // 1024,)),
            pltpu.SemaphoreType.DMA,
            pltpu.SemaphoreType.DMA((n_chunks,)),
            pltpu.SemaphoreType.REGULAR((2, n_chunks)),
        ],
        compiler_params=pltpu.CompilerParams(collective_id=1, has_side_effects=True, vmem_limit_bytes=67043328),
    )(o, g_attn.reshape(1, -1), g_mlp.reshape(1, -1), x_seq.reshape(n_chunks, 8, blk, d_model), w_o, w1, w3, w2)
    return y.reshape(n_chunks, rows, d_model)


def rope_tables(positions, head_dim):
    half_dim = head_dim // 2
    inv_freq = ROPE_THETA ** (-(jnp.arange(half_dim, dtype=F32) * (2.0 / head_dim)))
    angles = positions.astype(F32)[:, None] * inv_freq[None, :]
    return jnp.cos(angles), jnp.sin(angles)


def apply_rope(head_vals, cos_tab, sin_tab):
    half_dim = head_vals.shape[-1] // 2
    lead = head_vals[..., :half_dim]
    tail_half = head_vals[..., half_dim:]
    cos_rows = cos_tab[:, None, :]
    sin_rows = sin_tab[:, None, :]
    return jnp.concatenate([lead * cos_rows - tail_half * sin_rows, tail_half * cos_rows + lead * sin_rows], axis=-1)


def local_layer(tp_size, x_seq, cache_len, k_cache, v_cache, w_q, w_k, w_v, w_o, w_gate, w_up, w_down, g_q, g_k, g_attn, g_mlp):
    n_steps, n_rows, d_model = x_seq.shape
    seq_max, head_dim = k_cache.shape[2:]
    q_loc = w_q.shape[1]
    heads = q_loc // head_dim
    x_all = x_seq.reshape(n_steps * n_rows, d_model)
    q_raw = jnp.dot(x_all, w_q, preferred_element_type=F32).astype(BF16).astype(F32)
    k_raw = jnp.dot(x_all, w_k, preferred_element_type=F32).astype(BF16).astype(F32)
    v_new = jnp.dot(x_all, w_v, preferred_element_type=F32).astype(BF16)
    sq = jnp.stack([jnp.sum(q_raw * q_raw, axis=-1), jnp.sum(k_raw * k_raw, axis=-1)])
    sq = lax.psum(sq, 'tp')
    pos = (jnp.arange(n_steps, dtype=jnp.int32)[:, None] + cache_len[None, :]).reshape(-1)
    cos_tab, sin_tab = rope_tables(pos, head_dim)
    q_n = (q_raw * rms_factor(sq[0], q_loc * tp_size)[:, None] * g_q.astype(F32)).reshape(-1, heads, head_dim)
    k_n = (k_raw * rms_factor(sq[1], head_dim * tp_size)[:, None] * g_k.astype(F32)).reshape(-1, 1, head_dim)
    q_rot = apply_rope(q_n, cos_tab, sin_tab).astype(BF16).reshape(n_steps, n_rows, heads, head_dim)
    k_rot = apply_rope(k_n, cos_tab, sin_tab).astype(BF16).reshape(n_steps, n_rows, head_dim)
    v_rot = v_new.reshape(n_steps, n_rows, head_dim)
    slot = jnp.arange(seq_max, dtype=jnp.int32)[None, :, None] - cache_len[:, None, None]
    k_out, v_out = k_cache[:, 0], v_cache[:, 0]
    for t in range(n_steps):
        k_out = jnp.where(slot == t, k_rot[t][:, None, :], k_out)
        v_out = jnp.where(slot == t, v_rot[t][:, None, :], v_out)
    q_seq = q_rot.transpose(1, 0, 2, 3).reshape(n_rows, n_steps * heads, head_dim)
    s = jnp.einsum('bqd,bsd->bqs', q_seq, k_out, preferred_element_type=F32) * head_dim ** -0.5
    limit = cache_len[:, None] + jnp.repeat(jnp.arange(n_steps, dtype=jnp.int32), heads)[None, :]
    s = jnp.where(jnp.arange(seq_max)[None, None, :] <= limit[:, :, None], s, -jnp.inf)
    e = jnp.exp(s - jnp.max(s, axis=-1, keepdims=True))
    l = jnp.sum(e, axis=-1, keepdims=True)
    o = jnp.einsum('bqs,bsd->bqd', e.astype(BF16), v_out, preferred_element_type=F32)
    o = (o / l).astype(BF16).reshape(n_rows, n_steps, q_loc).transpose(1, 0, 2)
    y = tail(o, x_seq, w_o, w_gate, w_up, w_down, g_attn, g_mlp)
    return y, k_out[:, None], v_out[:, None]


def solution(mesh):
    tp_size = mesh.shape['tp']
    data_spec = P(None, 'dp', None)
    cache_spec = P('dp', 'tp', None, None)
    col_spec = P(None, 'tp')
    row_spec = P('tp', None)
    arg_specs = (data_spec, P('dp'), cache_spec, cache_spec, col_spec, col_spec, col_spec, row_spec, col_spec, col_spec, row_spec, P('tp'), P('tp'), P(None), P(None))
    out_specs = (data_spec, cache_spec, cache_spec)
    return jax.shard_map(functools.partial(local_layer, tp_size), mesh=mesh, in_specs=arg_specs, out_specs=out_specs, check_vma=False)
```

time: 345 us -> 289 us (0.84); the launches traced: 339 us -> 287 us
  Pallas kernels: 0 us -> 127 us
  waiting for transfers between devices: 118 us -> 0 us
  matrix products: 138 us -> 67.3 us
  local copies, waits for them, and re-layouts: 8.27 us -> 53.1 us
  other arithmetic: 44.4 us -> 23.4 us
  between operations: 15.1 us -> 1.1 us
    pallas_call x0 -> x1, Pallas kernels: none -> 127 us  [tail(): pl.pallas_call(functools.partial(tail_kernel, dims), name='tail', out_sha...]
    psum x2 -> x0, waiting for transfers between devices: 118 us -> none  [group_psum(): return lax.psum(part_val, 'tp')]
    dot_general x29 -> x5, matrix products: 138 us -> 67.3 us  [the longest x1 31.6 us: local_layer(): jnp.einsum('bqd,bsd->bqs', q_seq, k_out, preferred_element_type=F32)]
    unnamed x108 -> x45, local copies, waits for them, and re-layouts: 4.55 us -> 48.5 us
    reduce_sum x11 -> x1, other arithmetic: 11.9 us -> 0.69 us  [local_layer(): l = jnp.sum(e, axis=-1, keepdims=True)]
    another operation x11 -> x3, other arithmetic: 7.62 us -> 0.59 us  [the longest x2 5.41 us: layer_steps(): return (jnp.stack(y_list), k_out, v_out)]
    convert_element_type x6 -> x3, other arithmetic: 4.87 us -> 0.01 us  [the longest x1 0.01 us: rope_tables(): angles = positions.astype(F32)[:, None] * inv_freq[None, :]]
  transfers between devices with their start and end apart: 2 -> 0, of which waited for: 2 -> 0; matrix products, arithmetic and copies ran while one was open for 6% -> 0% of each run, Pallas kernels for 0% -> 0%
where the time goes in v1:
time: 289 us; the launch traced here: 287 us
  Pallas kernels  127 us (44%)
  matrix products  67.3 us (23%)
  local copies, waits for them, and re-layouts  53.1 us (18%)
  other arithmetic  23.4 us (8%)
  blocking collectives  15.6 us (5%)
    pallas_call x1, Pallas kernels, tail(): pl.pallas_call(functools.partial(tail_kernel, dims), name='tail', out_sha...  127 us
    unnamed x45, local copies, waits for them, and re-layouts  48.5 us
    dot_general x1, matrix products, local_layer(): jnp.einsum('bqd,bsd->bqs', q_seq, k_out, preferred_element_type=F32)  31.6 us
    dot_general x1, matrix products, local_layer(): jnp.einsum('bqs,bsd->bqd', e.astype(BF16), v_out, preferred_element_type=...  25.8 us
    select_n x1, other arithmetic, local_layer(): v_out = jnp.where(slot == t, v_rot[t][:, None, :], v_out)  20.8 us
    psum x1, blocking collectives, local_layer(): sq = lax.psum(sq, 'tp')  15.6 us
    dot_general x1, matrix products, local_layer(): jnp.dot(x_all, w_q, preferred_element_type=F32).astype(BF16).astype(F32)  7.47 us

profile of v1, /device:TPU:0, one launch (start us, length us, event | category | flops | bytes accessed | tf_op | source)
XLA Modules:
  0.0 287.3 jit_solution(12330386573108360177)
XLA Ops:
  0.6 0.0 copy-start
  0.7 7.5 %multiply_reduce_fusion = (f32[384]{0:T(512)S(1)}, f32[384,640]{1,0:T(8,128)S(1)}) fusion(bf16[384,5120]{1,0:T(8,128)(2,1)} %bitcast.54, bf16[5120,640]{1,0:T(8,128)(2,1)} %param.19), kind=kOutput, calls=%fused_computation.35 | convolution fusion | flops 2517564928 | bytes 11470336 | tf_op jit(solution)/shard_map/dot_general | solution.py:376
  8.1 0.0 copy-start.16
  8.2 0.0 copy-done
  8.2 0.0 copy-done.3
  8.2 0.0 copy-start.18
  8.2 1.2 multiply_reduce_fusion.1
  9.5 15.6 %psum.7 = f32[2,384]{1,0:T(2,128)S(1)} all-reduce(f32[2,384]{1,0:T(2,128)S(1)} %pad_maximum_fusion.1), channel_id=1, replica_groups=mesh['dp'=2,'tp'=8] {'tp'}, use_global_device_ids=true, to_apply=%region_2.0 | all-reduce | flops 768 | bytes 6144 | tf_op jit(solution)/shard_map/psum | solution.py:380
  25.1 0.0 copy-done.17
  25.1 0.1 multiply_multiply_fusion
  25.3 0.3 copy.42
  25.6 0.0 copy-done.16
  25.6 0.4 multiply_cosine_fusion.1
  26.1 0.1 subtract_convert_fusion
  26.2 0.1 concatenate.21
  26.3 0.1 concatenate.22
  26.3 0.4 maximum_bitcast_fusion
  26.8 0.9 copy.43
  27.7 0.1 multiply_bitcast_fusion
  27.8 0.4 fusion.41
  28.3 0.1 copy.44
  28.4 0.1 copy.45
  28.6 0.1 copy.46
  28.7 0.1 fusion.39
  28.9 0.1 add.63
  28.9 0.1 broadcast_add_fusion
  29.0 0.0 copy-start.1
  29.0 0.0 copy-start.4
  29.1 0.0 slice-start.1
  29.1 31.6 %fusion.56 = (f32[128,15]{1,0:T(8,128)S(1)}, f32[128,15,256]{2,1,0:T(8,128)S(1)}) fusion(bf16[128,1,256,128]{3,2,1,0:T(8,128)(2,1)} %param.17, pred[128,256]{1,0:T(8,128)(4,1)S(1)} %get-tuple-element.20, pred[128,256]{1,0:T(8,128)(4,1)S(1)} %get-tuple-element.21, pred[128,256]{1,0:T(8,128)(4,1)S(1)} %get-tuple-element.19, bf16[128,128]{1,0:T(8,128)(2,1)S(1)} %copy.46, ...), kind=kOutput, calls=%fused_computation.81 | convolution fusion | flops 140376192 | bytes 11058176 | tf_op jit(solution)/shard_map/bqd,bsd->bqs/dot_general | solution.py:394
  60.6 0.0 copy-done.8
  60.6 0.0 copy-done.9
  60.7 0.0 copy-done.10
  60.7 0.7 fusion.20
  61.4 1.2 convolution_convert_fusion.1
  62.6 0.5 copy-done.11
  63.2 0.0 copy-done.12
  63.2 0.0 copy-done.13
  63.2 25.8 %divide_convert_fusion = bf16[128,15,128]{2,1,0:T(8,128)(2,1)S(1)} fusion(bf16[128,1,256,128]{3,2,1,0:T(8,128)(2,1)S(1)} %bitcast.60, pred[128,256]{1,0:T(8,128)(4,1)S(1)} %get-tuple-element.20, pred[128,256]{1,0:T(8,128)(4,1)S(1)} %get-tuple-element.21, pred[128,256]{1,0:T(8,128)(4,1)S(1)} %get-tuple-element.19, ...), kind=kOutput, calls=%fused_computation.32 | convolution fusion | flops 139886592 | bytes 11058176 | tf_op jit(solution)/shard_map/bqs,bsd->bqd/dot_general | solution.py:399
  89.0 0.5 copy.48
  89.5 1.0 copy.49
  90.5 22.9 %copy.50.w1_hbm = bf16[5120,1728]{1,0:T(8,128)(2,1)} copy(bf16[5120,1728]{0,1:T(8,128)(2,1)} %param.23) | data formatting | bytes 35389440 | tf_op args[8]
  113.4 23.0 %copy.51.w3_hbm = bf16[5120,1728]{1,0:T(8,128)(2,1)} copy(bf16[5120,1728]{0,1:T(8,128)(2,1)} %param.24) | data formatting | bytes 35389440 | tf_op args[9]
  136.4 0.6 reshape.326.ga_ref
  137.1 0.6 reshape.327.gm_ref
  137.7 126.8 %tail.1 = bf16[3,8,16,5120]{3,2,1,0:T(8,128)(2,1)} custom-call(bf16[3,128,640]{2,1,0:T(8,128)(2,1)} %bitcast.62, bf16[1,5120]{1,0:T(2,128)(2,1)} %reshape.326.ga_ref, bf16[1,5120]{1,0:T(2,128)(2,1)} %reshape.327.gm_ref, bf16[3,8,16,5120]{3,2,1,0:T(8,128)(2,1)} %bitcast.55, bf16[640,5120]{1,0:T(8,128)(2,1)} %wo_hbm.1, bf16[5120,1728]{1,0:T(8,128)(2,1)} %copy.50.w1_hbm, ...), custom_call_target="tpu_custom_call" | custom-call | tf_op jit(solution)/shard_map/tail/pallas_call | solution.py:324
  264.6 20.8 %select_select_fusion = (bf16[128,1,256,128]{3,2,1,0:T(8,128)(2,1)}, bf16[128,1,256,128]{3,2,1,0:T(8,128)(2,1)}) fusion(bf16[128,1,256,128]{3,2,1,0:T(8,128)(2,1)} %param.18, pred[128,256]{1,0:T(8,128)(4,1)} %copy-done.6, pred[128,256]{1,0:T(8,128)(4,1)} %copy-done.7, pred[128,256]{1,0:T(8,128)(4,1)} %copy-done.5, bf16[128,128]{1,0:T(8,128)(2,1)} %copy-done.12, ...), kind=kLoop, calls=%fused_computation.7 | loop fusion | flops 25165824 | bytes 33849344 | tf_op jit(solution)/shard_map/jit(_where)/select_n | solution.py:392
  285.3 1.9 copy.61
  (38 shorter events, 0.2 us)
Async XLA Ops:
  0.6 7.5 %copy-start = (bf16[3,128,5120]{2,1,0:T(8,128)(2,1)S(1)}, bf16[3,128,5120]{2,1,0:T(8,128)(2,1)}, u32[]{:S(2)}) copy-start(bf16[3,128,5120]{2,1,0:T(8,128)(2,1)} %param.15) | copy-start | bytes 11796484
  0.6 7.5 %copy-start.3 = (bf16[5120,128]{1,0:T(8,128)(2,1)S(1)}, bf16[5120,128]{1,0:T(8,128)(2,1)}, u32[]{:S(2)}) copy-start(bf16[5120,128]{1,0:T(8,128)(2,1)} %param.20) | copy-start | bytes 3932164
  8.1 17.0 %copy-start.17 = (bf16[640]{0:T(1024)(128)(2,1)S(1)}, bf16[640]{0:T(1024)(128)(2,1)}, u32[]{:S(2)}) copy-start(bf16[640]{0:T(1024)(128)(2,1)} %param.26) | copy-start | bytes 3844
  8.1 17.5 %copy-start.16 = (s32[128]{0:T(128)S(1)}, s32[128]{0:T(128)}, u32[]{:S(2)}) copy-start(s32[128]{0:T(128)} %param.16) | copy-start | bytes 1540
  8.2 19.5 %copy-start.18 = (bf16[128]{0:T(256)(128)(2,1)S(1)}, bf16[128]{0:T(256)(128)(2,1)}, u32[]{:S(2)}) copy-start(bf16[128]{0:T(256)(128)(2,1)} %param.27) | copy-start | bytes 772
  28.4 32.2 %copy-start.8 = (bf16[128,128]{1,0:T(8,128)(2,1)}, bf16[128,128]{1,0:T(8,128)(2,1)S(1)}, u32[]{:S(2)}) copy-start(bf16[128,128]{1,0:T(8,128)(2,1)S(1)} %copy.44) | copy-start | bytes 98308
  28.5 32.1 %copy-start.9 = (bf16[128,128]{1,0:T(8,128)(2,1)}, bf16[128,128]{1,0:T(8,128)(2,1)S(1)}, u32[]{:S(2)}) copy-start(bf16[128,128]{1,0:T(8,128)(2,1)S(1)} %copy.45) | copy-start | bytes 98308
  28.7 32.0 %copy-start.10 = (bf16[128,128]{1,0:T(8,128)(2,1)}, bf16[128,128]{1,0:T(8,128)(2,1)S(1)}, u32[]{:S(2)}) copy-start(bf16[128,128]{1,0:T(8,128)(2,1)S(1)} %copy.46) | copy-start | bytes 98308
  28.8 33.8 %copy-start.5 = (pred[128,256]{1,0:T(8,128)(4,1)}, pred[128,256]{1,0:T(8,128)(4,1)S(1)}, u32[]{:S(2)}) copy-start(pred[128,256]{1,0:T(8,128)(4,1)S(1)} %get-tuple-element.19) | copy-start | bytes 98308
  28.8 33.8 %copy-start.6 = (pred[128,256]{1,0:T(8,128)(4,1)}, pred[128,256]{1,0:T(8,128)(4,1)S(1)}, u32[]{:S(2)}) copy-start(pred[128,256]{1,0:T(8,128)(4,1)S(1)} %get-tuple-element.20) | copy-start | bytes 98308
  28.8 33.8 %copy-start.7 = (pred[128,256]{1,0:T(8,128)(4,1)}, pred[128,256]{1,0:T(8,128)(4,1)S(1)}, u32[]{:S(2)}) copy-start(pred[128,256]{1,0:T(8,128)(4,1)S(1)} %get-tuple-element.21) | copy-start | bytes 98308
  28.9 34.3 %slice-start = ((s8[8388608]{0:T(1024)(128)(4,1)}), s8[4194304]{0:T(1024)(128)(4,1)S(1)}, s32[]{:S(2)}) async-start(s8[8388608]{0:T(1024)(128)(4,1)} %bitcast.59), calls=%async_computation | async-start | bytes 8388608
  29.0 32.3 %copy-start.1 = (bf16[3,128,5120]{2,1,0:T(8,128)(2,1)S(1)}, bf16[3,128,5120]{2,1,0:T(8,128)(2,1)}, u32[]{:S(2)}) copy-start(bf16[3,128,5120]{2,1,0:T(8,128)(2,1)} %param.15) | copy-start | bytes 11796484
  29.0 32.3 %copy-start.4 = (bf16[5120,128]{1,0:T(8,128)(2,1)S(1)}, bf16[5120,128]{1,0:T(8,128)(2,1)}, u32[]{:S(2)}) copy-start(bf16[5120,128]{1,0:T(8,128)(2,1)} %param.21) | copy-start | bytes 3932164
  29.1 34.2 %slice-start.1 = ((s8[8388608]{0:T(1024)(128)(4,1)}), s8[4194304]{0:T(1024)(128)(4,1)S(1)}, s32[]{:S(2)}) async-start(s8[8388608]{0:T(1024)(128)(4,1)} %bitcast.59), calls=%async_computation.1 | async-start | bytes 8388608
  62.6 0.6 copy-start.11
  62.6 0.6 copy-start.12
  62.6 0.6 copy-start.13
  113.4 23.0 %copy-start.14 = (bf16[5120]{0:T(1024)(128)(2,1)S(1)}, bf16[5120]{0:T(1024)(128)(2,1)}, u32[]{:S(2)}) copy-start(bf16[5120]{0:T(1024)(128)(2,1)} %param.28) | copy-start | bytes 30724
  113.4 23.6 %copy-start.15 = (bf16[5120]{0:T(1024)(128)(2,1)S(1)}, bf16[5120]{0:T(1024)(128)(2,1)}, u32[]{:S(2)}) copy-start(bf16[5120]{0:T(1024)(128)(2,1)} %param.29) | copy-start | bytes 30724
  264.5 20.8 %copy-start.2 = (bf16[3,8,16,5120]{3,2,1,0:T(8,128)(2,1)S(1)}, bf16[3,8,16,5120]{3,2,1,0:T(8,128)(2,1)}, u32[]{:S(2)}) copy-start(bf16[3,8,16,5120]{3,2,1,0:T(8,128)(2,1)} %tail.1) | copy-start | bytes 11796484

commit v2 on v1

--- a/solution.py
+++ b/solution.py
@@ -49,7 +49,7 @@
         return pltpu.make_async_copy(x_hbm.at[:, me], own, x_sem)
 
     n_k = 4
-    k_rows = d_model // n_k
+    k_rows = ff_loc // n_k
 
     def w13_copy(i, j):
         src, dst = ((w1_hbm, w1), (w3_hbm, w3))[i]
@@ -215,10 +215,13 @@
     dn_tile = 512
     n_dn = d_model // dn_tile
 
+    def dot_t(lhs, rhs):
+        return lax.dot_general(lhs, rhs, (((1,), (1,)), ((), ())), preferred_element_type=F32)
+
     def gate_up(c, cs, width):
         h = buf[c].reshape(rows, d_model)
-        gate = jnp.dot(h, w1[:, cs], preferred_element_type=F32)
-        up = jnp.dot(h, w3[:, cs], preferred_element_type=F32)
+        gate = dot_t(h, w1[cs, :])
+        up = dot_t(h, w3[cs, :])
         act[:, cs] = (gate * jax.nn.sigmoid(gate) * up).astype(BF16)
 
     def p2(services):
@@ -316,7 +319,7 @@
 def tail(o, x_seq, w_o, w1, w3, w2, g_attn, g_mlp):
     n_chunks, rows, d_model = x_seq.shape
     q_loc = o.shape[-1]
-    ff_loc = w1.shape[1]
+    ff_loc = w2.shape[0]
     blk = rows // 8
     dims = (n_chunks, rows, d_model, q_loc, ff_loc)
     vmem = pl.BlockSpec(memory_space=pltpu.VMEM)
@@ -335,8 +338,8 @@
             pltpu.VMEM((n_chunks, blk, d_model), BF16),
             pltpu.VMEM((n_chunks, blk, d_model), BF16),
             pltpu.VMEM((rows, ff_loc), BF16),
-            pltpu.VMEM((d_model, ff_loc), BF16),
-            pltpu.VMEM((d_model, ff_loc), BF16),
+            pltpu.VMEM((ff_loc, d_model), BF16),
+            pltpu.VMEM((ff_loc, d_model), BF16),
             pltpu.VMEM((ff_loc, d_model), BF16),
             pltpu.SemaphoreType.DMA((2, n_chunks, 12)),
             pltpu.SemaphoreType.DMA((2, n_chunks, 12)),
@@ -347,57 +350,184 @@
             pltpu.SemaphoreType.REGULAR((2, n_chunks)),
         ],
         compiler_params=pltpu.CompilerParams(collective_id=1, has_side_effects=True, vmem_limit_bytes=67043328),
-    )(o, g_attn.reshape(1, -1), g_mlp.reshape(1, -1), x_seq.reshape(n_chunks, 8, blk, d_model), w_o, w1, w3, w2)
+    )(o, g_attn.reshape(1, -1), g_mlp.reshape(1, -1), x_seq.reshape(n_chunks, 8, blk, d_model), w_o, w1.T, w3.T, w2)
     return y.reshape(n_chunks, rows, d_model)
 
 
-def rope_tables(positions, head_dim):
-    half_dim = head_dim // 2
-    inv_freq = ROPE_THETA ** (-(jnp.arange(half_dim, dtype=F32) * (2.0 / head_dim)))
-    angles = positions.astype(F32)[:, None] * inv_freq[None, :]
-    return jnp.cos(angles), jnp.sin(angles)
-
-
-def apply_rope(head_vals, cos_tab, sin_tab):
-    half_dim = head_vals.shape[-1] // 2
-    lead = head_vals[..., :half_dim]
-    tail_half = head_vals[..., half_dim:]
-    cos_rows = cos_tab[:, None, :]
-    sin_rows = sin_tab[:, None, :]
-    return jnp.concatenate([lead * cos_rows - tail_half * sin_rows, tail_half * cos_rows + lead * sin_rows], axis=-1)
-
-
-def local_layer(tp_size, x_seq, cache_len, k_cache, v_cache, w_q, w_k, w_v, w_o, w_gate, w_up, w_down, g_q, g_k, g_attn, g_mlp):
-    n_steps, n_rows, d_model = x_seq.shape
-    seq_max, head_dim = k_cache.shape[2:]
-    q_loc = w_q.shape[1]
-    heads = q_loc // head_dim
-    x_all = x_seq.reshape(n_steps * n_rows, d_model)
-    q_raw = jnp.dot(x_all, w_q, preferred_element_type=F32).astype(BF16).astype(F32)
-    k_raw = jnp.dot(x_all, w_k, preferred_element_type=F32).astype(BF16).astype(F32)
-    v_new = jnp.dot(x_all, w_v, preferred_element_type=F32).astype(BF16)
-    sq = jnp.stack([jnp.sum(q_raw * q_raw, axis=-1), jnp.sum(k_raw * k_raw, axis=-1)])
-    sq = lax.psum(sq, 'tp')
-    pos = (jnp.arange(n_steps, dtype=jnp.int32)[:, None] + cache_len[None, :]).reshape(-1)
-    cos_tab, sin_tab = rope_tables(pos, head_dim)
-    q_n = (q_raw * rms_factor(sq[0], q_loc * tp_size)[:, None] * g_q.astype(F32)).reshape(-1, heads, head_dim)
-    k_n = (k_raw * rms_factor(sq[1], head_dim * tp_size)[:, None] * g_k.astype(F32)).reshape(-1, 1, head_dim)
-    q_rot = apply_rope(q_n, cos_tab, sin_tab).astype(BF16).reshape(n_steps, n_rows, heads, head_dim)
-    k_rot = apply_rope(k_n, cos_tab, sin_tab).astype(BF16).reshape(n_steps, n_rows, head_dim)
-    v_rot = v_new.reshape(n_steps, n_rows, head_dim)
-    slot = jnp.arange(seq_max, dtype=jnp.int32)[None, :, None] - cache_len[:, None, None]
-    k_out, v_out = k_cache[:, 0], v_cache[:, 0]
+def head_kernel(dims, len_ref, gq_ref, gk_ref, freq_ref, x_hbm, wq_hbm, wk_hbm, wv_hbm, q_out, k_out, v_out,
+                x, w, raw, cos_t, sin_t, sums, x_sem, w_sem, send_sem, recv_sem):
+    n_steps, rows, d_model, q_loc, hd, n_tp = dims
+    heads = q_loc // hd
+    width = q_loc + 2 * hd
+    tp = lax.axis_index('tp')
+
+    def x_copy(t):
+        return pltpu.make_async_copy(x_hbm.at[t], x.at[t], x_sem.at[t])
+
+    n_k = 4
+    k_rows = d_model // n_k
+
+    def w_copies(j):
+        rs = pl.ds(j * k_rows, k_rows)
+        return (pltpu.make_async_copy(wq_hbm.at[rs], w.at[rs, pl.ds(0, q_loc)], w_sem.at[0, j]),
+                pltpu.make_async_copy(wk_hbm.at[rs], w.at[rs, pl.ds(q_loc, hd)], w_sem.at[1, j]),
+                pltpu.make_async_copy(wv_hbm.at[rs], w.at[rs, pl.ds(q_loc + hd, hd)], w_sem.at[2, j]))
+
+    x_copy(0).start()
+    for j in range(n_k):
+        for cp in w_copies(j):
+            cp.start()
+    for t in range(1, n_steps):
+        x_copy(t).start()
+
+    barrier = pltpu.get_barrier_semaphore()
+    peers = [lax.rem(tp + d, n_tp) for d in range(1, n_tp)]
+    for p in peers:
+        pl.semaphore_signal(barrier, inc=1, device_id={'tp': p}, device_id_type=pl.DeviceIdType.MESH)
+
+    lens = jnp.transpose(jnp.broadcast_to(len_ref[...].astype(F32), (rows, rows)))
+    lane = lax.broadcasted_iota(jnp.int32, (rows, hd), 1)
+    sign = jnp.where(lane < hd // 2, -1.0, 1.0).astype(F32)
     for t in range(n_steps):
-        k_out = jnp.where(slot == t, k_rot[t][:, None, :], k_out)
-        v_out = jnp.where(slot == t, v_rot[t][:, None, :], v_out)
-    q_seq = q_rot.transpose(1, 0, 2, 3).reshape(n_rows, n_steps * heads, head_dim)
-    s = jnp.einsum('bqd,bsd->bqs', q_seq, k_out, preferred_element_type=F32) * head_dim ** -0.5
-    limit = cache_len[:, None] + jnp.repeat(jnp.arange(n_steps, dtype=jnp.int32), heads)[None, :]
-    s = jnp.where(jnp.arange(seq_max)[None, None, :] <= limit[:, :, None], s, -jnp.inf)
-    e = jnp.exp(s - jnp.max(s, axis=-1, keepdims=True))
-    l = jnp.sum(e, axis=-1, keepdims=True)
-    o = jnp.einsum('bqs,bsd->bqd', e.astype(BF16), v_out, preferred_element_type=F32)
-    o = (o / l).astype(BF16).reshape(n_rows, n_steps, q_loc).transpose(1, 0, 2)
+        ang = (lens + float(t)) * freq_ref[...]
+        cos_t[t] = jnp.cos(ang)
+        sin_t[t] = jnp.sin(ang) * sign
+
+    for j in range(n_k):
+        for cp in w_copies(j):
+            cp.wait()
+    part = jnp.zeros((rows, rows), F32)
+    sq_lane = lax.broadcasted_iota(jnp.int32, (rows, rows), 1)
+    for t in range(n_steps):
+        x_copy(t).wait()
+        res = jnp.dot(x[t], w[...], preferred_element_type=F32).astype(BF16)
+        raw[t] = res
+        q = res[:, :q_loc].astype(F32)
+        k = res[:, q_loc:q_loc + hd].astype(F32)
+        part = jnp.where(sq_lane == 2 * t, jnp.sum(q * q, axis=-1, keepdims=True), part)
+        part = jnp.where(sq_lane == 2 * t + 1, jnp.sum(k * k, axis=-1, keepdims=True), part)
+    sums[tp] = jnp.transpose(part)[0:8]
+    pl.semaphore_wait(barrier, n_tp - 1)
+
+    def send(d):
+        return pltpu.make_async_remote_copy(
+            src_ref=sums.at[tp], dst_ref=sums.at[tp], send_sem=send_sem.at[d], recv_sem=recv_sem.at[d],
+            device_id={'tp': peers[d]}, device_id_type=pl.DeviceIdType.MESH)
+
+    for d in range(n_tp - 1):
+        send(d).start()
+    q_out[pl.ds(n_steps * heads, rows, stride=16), :] = jnp.zeros((rows, hd), F32)
+    for t in range(n_steps):
+        v_out[t] = raw[t, :, q_loc + hd:width].astype(F32)
+    for d in range(n_tp - 1):
+        send(d).wait()
+    tot = sums[0]
+    for d in range(1, n_tp):
+        tot = tot + sums[d]
+    full = jnp.transpose(jnp.concatenate([tot, jnp.zeros((rows - 8, rows), F32)], axis=0))
+    for t in range(n_steps):
+        q_scale = rms_factor(full[:, 2 * t:2 * t + 1], q_loc * n_tp)
+        k_scale = rms_factor(full[:, 2 * t + 1:2 * t + 2], hd * n_tp)
+
+        def rotate(col, scale, gain):
+            val = raw[t, :, col:col + hd].astype(F32) * scale * gain.astype(F32)
+            return (val * cos_t[t] + pltpu.roll(val, hd // 2, 1) * sin_t[t]).astype(BF16).astype(F32)
+        for j in range(heads):
+            q_out[pl.ds(t * heads + j, rows, stride=16), :] = rotate(j * hd, q_scale, gq_ref[:, j * hd:(j + 1) * hd])
+        k_out[t] = rotate(q_loc, k_scale, gk_ref[...])
+
+
+def head(x_seq, cache_len, w_q, w_k, w_v, g_q, g_k, n_tp):
+    n_steps, rows, d_model = x_seq.shape
+    q_loc, hd = w_q.shape[1], w_k.shape[1]
+    width = q_loc + 2 * hd
+    half = hd // 2
+    inv_freq = ROPE_THETA ** (-(jnp.arange(half, dtype=F32) * (2.0 / hd)))
+    freq = jnp.concatenate([inv_freq, inv_freq]).reshape(1, hd)
+    vmem = pl.BlockSpec(memory_space=pltpu.VMEM)
+    hbm = pl.BlockSpec(memory_space=pl.ANY)
+    return pl.pallas_call(
+        functools.partial(head_kernel, (n_steps, rows, d_model, q_loc, hd, n_tp)),
+        name='head',
+        out_shape=(jax.ShapeDtypeStruct((rows * 16, hd), F32),
+                   jax.ShapeDtypeStruct((n_steps, rows, hd), F32),
+                   jax.ShapeDtypeStruct((n_steps, rows, hd), F32)),
+        in_specs=[vmem] * 4 + [hbm] * 4,
+        out_specs=(vmem,) * 3,
+        scratch_shapes=[
+            pltpu.VMEM((n_steps, rows, d_model), BF16),
+            pltpu.VMEM((d_model, width), BF16),
+            pltpu.VMEM((n_steps, rows, width), BF16),
+            pltpu.VMEM((n_steps, rows, hd), F32),
+            pltpu.VMEM((n_steps, rows, hd), F32),
+            pltpu.VMEM((n_tp, 8, rows), F32),
+            pltpu.SemaphoreType.DMA((n_steps,)),
+            pltpu.SemaphoreType.DMA((3, 4)),
+            pltpu.SemaphoreType.DMA((n_tp - 1,)),
+            pltpu.SemaphoreType.DMA((n_tp - 1,)),
+        ],
+        compiler_params=pltpu.CompilerParams(collective_id=0, has_side_effects=True, vmem_limit_bytes=67043328),
+    )(cache_len.reshape(1, -1), g_q.reshape(1, -1), g_k.reshape(1, -1), freq, x_seq, w_q, w_k, w_v)
+
+
+def attn_kernel(dims, len_ref, q_ref, kn_ref, vn_ref, k_ref, v_ref, o_ref, ko_ref, vo_ref, o_scr):
+    n_steps, nb, heads, hd, seq_max = dims
+    first = pl.program_id(0) * nb
+    win = 32
+    row_step = lax.broadcasted_iota(jnp.int32, (16, seq_max), 0) // heads
+    col = lax.broadcasted_iota(jnp.int32, (16, seq_max), 1)
+    ahead = col - row_step
+    win_row = lax.broadcasted_iota(jnp.int32, (win, hd), 0)
+    for i in range(nb):
+        ln = len_ref[first + i]
+        base = pl.multiple_of(jnp.minimum((ln // 16) * 16, seq_max - win), 16)
+        rel = win_row + (base - ln)
+        for src, new, dst in ((k_ref, kn_ref, ko_ref), (v_ref, vn_ref, vo_ref)):
+            dst[i] = src[i]
+            cut = src[i, pl.ds(base, win), :].astype(F32)
+            for t in range(n_steps):
+                cut = jnp.where(rel == t, new[t, i:i + 1, :], cut)
+            dst[i, pl.ds(base, win), :] = cut.astype(BF16)
+        q = q_ref[i].astype(BF16)
+        s = lax.dot_general(q, ko_ref[i], (((1,), (1,)), ((), ())), preferred_element_type=F32) * hd ** -0.5
+        s = jnp.where(ahead <= ln, s, -jnp.inf)
+        e = jnp.exp(s - jnp.max(s, axis=-1, keepdims=True))
+        l = jnp.sum(e, axis=-1, keepdims=True)
+        o = jnp.dot(e.astype(BF16), vo_ref[i], preferred_element_type=F32) / l
+        o_scr[i * 16:(i + 1) * 16, :] = o
+    for t in range(n_steps):
+        for j in range(heads):
+            o_ref[t, :, j * hd:(j + 1) * hd] = o_scr[pl.ds(t * heads + j, nb, stride=16), :].astype(BF16)
+
+
+def attend(q, kn, vn, k_cache, v_cache, cache_len, heads):
+    n_rows, _, seq_max, hd = k_cache.shape
+    n_steps = kn.shape[0]
+    nb = 16
+    cache_spec = pl.BlockSpec((nb, seq_max, hd), lambda i, ln: (i, 0, 0))
+    new_spec = pl.BlockSpec((n_steps, nb, hd), lambda i, ln: (0, i, 0))
+    cache_shape = jax.ShapeDtypeStruct((n_rows, seq_max, hd), BF16)
+    flops = 4 * n_rows * 16 * seq_max * hd
+    return pl.pallas_call(
+        functools.partial(attn_kernel, (n_steps, nb, heads, hd, seq_max)),
+        name='attend',
+        grid_spec=pltpu.PrefetchScalarGridSpec(
+            num_scalar_prefetch=1,
+            grid=(n_rows // nb,),
+            in_specs=[pl.BlockSpec((nb, 16, hd), lambda i, ln: (i, 0, 0)), new_spec, new_spec, cache_spec, cache_spec],
+            out_specs=(pl.BlockSpec((n_steps, nb, heads * hd), lambda i, ln: (0, i, 0)), cache_spec, cache_spec),
+            scratch_shapes=[pltpu.VMEM((nb * 16, hd), F32)],
+        ),
+        out_shape=(jax.ShapeDtypeStruct((n_steps, n_rows, heads * hd), BF16), cache_shape, cache_shape),
+        compiler_params=pltpu.CompilerParams(vmem_limit_bytes=67043328),
+        cost_estimate=pl.CostEstimate(flops=flops, bytes_accessed=4 * n_rows * seq_max * hd * 2, transcendentals=n_rows * 16 * seq_max),
+    )(cache_len, q.reshape(n_rows, 16, hd), kn, vn, k_cache[:, 0], v_cache[:, 0])
+
+
+def local_layer(n_tp, x_seq, cache_len, k_cache, v_cache, w_q, w_k, w_v, w_o, w_gate, w_up, w_down, g_q, g_k, g_attn, g_mlp):
+    heads = w_q.shape[1] // k_cache.shape[3]
+    q, kn, vn = head(x_seq, cache_len, w_q, w_k, w_v, g_q, g_k, n_tp)
+    o, k_out, v_out = attend(q, kn, vn, k_cache, v_cache, cache_len, heads)
     y = tail(o, x_seq, w_o, w_gate, w_up, w_down, g_attn, g_mlp)
     return y, k_out[:, None], v_out[:, None]
 

time: 289 us -> 204 us (0.71)
  matrix products: 67.3 us -> 0 us
  Pallas kernels: 127 us -> 194 us
  local copies, waits for them, and re-layouts: 53.1 us -> 8.17 us
  other arithmetic: 23.4 us -> 0.6 us
  blocking collectives: 15.6 us -> 0 us
    dot_general x5 -> x0, matrix products: 67.3 us -> none  [the longest x1 31.6 us: local_layer(): jnp.einsum('bqd,bsd->bqs', q_seq, k_out, preferred_element_type=F32)]
    pallas_call x0 -> x2, Pallas kernels: none -> 54.1 us  [the longest x1 35.7 us: attend(): pl.pallas_call(functools.partial(attn_kernel, (n_steps, nb, heads, hd, se...]
    unnamed x45 -> x1, local copies, waits for them, and re-layouts: 48.5 us -> 4.29 us
    select_n x1 -> x0, other arithmetic: 20.8 us -> none  [local_layer(): v_out = jnp.where(slot == t, v_rot[t][:, None, :], v_out)]
    psum x1 -> x0, blocking collectives: 15.6 us -> none  [local_layer(): sq = lax.psum(sq, 'tp')]
    pallas_call x1, Pallas kernels: 127 us -> 140 us  [tail(): pl.pallas_call(functools.partial(tail_kernel, dims), name='tail', out_sha...]
where the time goes in v2:
time: 204 us; the launch traced here: 203 us
  Pallas kernels  194 us (95%)
  local copies, waits for them, and re-layouts  8.17 us (4%)
    pallas_call x1, Pallas kernels, tail(): pl.pallas_call(functools.partial(tail_kernel, dims), name='tail', out_sha...  140 us
    pallas_call x1, Pallas kernels, attend(): pl.pallas_call(functools.partial(attn_kernel, (n_steps, nb, heads, hd, se...  35.7 us
    pallas_call x1, Pallas kernels, head(): pl.pallas_call(functools.partial(head_kernel, (n_steps, rows, d_model, q_...  18.4 us
    unnamed x1, local copies, waits for them, and re-layouts  4.29 us

profile of v2, /device:TPU:0, one launch (start us, length us, event | category | flops | bytes accessed | tf_op | source)
XLA Modules:
  0.0 203.2 jit_solution(1862898903913199881)
XLA Ops:
  0.6 0.6 maximum_bitcast_fusion.freq_ref
  1.2 1.3 reshape.34.gq_ref
  2.5 1.3 reshape.38.ga_ref
  3.8 1.3 reshape.39.gm_ref
  5.1 18.4 %head.1 = (f32[2048,128]{1,0:T(8,128)}, f32[3,128,128]{2,1,0:T(8,128)}, f32[3,128,128]{2,1,0:T(8,128)}) custom-call(s32[1,128]{1,0:T(1,128)} %bitcast.24, bf16[1,640]{1,0:T(2,128)(2,1)} %reshape.34.gq_ref, bf16[1,128]{1,0:T(2,128)(2,1)} %bitcast.25, f32[1,128]{1,0:T(1,128)} %maximum_bitcast_fusion.freq_ref, bf16[3,128,5120]{2,1,0:T(8,128)(2,1)} %x_hbm.1, ...), custom_call_target="tpu_custom_call" | custom-call | tf_op jit(solution)/shard_map/head/pallas_call | solution.py:449
  23.5 35.7 %attend.1 = (bf16[3,128,640]{2,1,0:T(8,128)(2,1)}, bf16[128,256,128]{2,1,0:T(8,128)(2,1)}, bf16[128,256,128]{2,1,0:T(8,128)(2,1)}) custom-call(s32[128]{0:T(128)} %len_ref.1, f32[128,16,128]{2,1,0:T(8,128)} %bitcast.23, f32[3,128,128]{2,1,0:T(8,128)} %get-tuple-element.10.kn_ref, f32[3,128,128]{2,1,0:T(8,128)} %get-tuple-element.11.vn_ref, ...), custom_call_target="tpu_custom_call" | custom-call | flops 268435456 | bytes 33554432 | tf_op jit(solution)/shard_map/attend/pallas_call | solution.py:511
  59.2 139.7 %tail.1 = bf16[3,8,16,5120]{3,2,1,0:T(8,128)(2,1)} custom-call(bf16[3,128,640]{2,1,0:T(8,128)(2,1)} %get-tuple-element.12.o_ref, bf16[1,5120]{1,0:T(2,128)(2,1)} %reshape.38.ga_ref, bf16[1,5120]{1,0:T(2,128)(2,1)} %reshape.39.gm_ref, bf16[3,8,16,5120]{3,2,1,0:T(8,128)(2,1)} %bitcast.19, bf16[640,5120]{1,0:T(8,128)(2,1)} %wo_hbm.1, ...), custom_call_target="tpu_custom_call" | custom-call | tf_op jit(solution)/shard_map/tail/pallas_call | solution.py:327
  198.9 4.3 %copy.21 = bf16[3,128,5120]{2,1,0:T(8,128)(2,1)} copy(bf16[3,128,5120]{2,1,0:T(8,128)(2,1)} %bitcast.20) | data formatting | bytes 7864320
  (1 shorter events, 0.0 us)

commit v3 on v2

v3 whole, which is shorter than its diff:
```python
import functools

import jax
import jax.numpy as jnp
import numpy as np
from jax import lax
from jax.experimental import pallas as pl
from jax.experimental.pallas import tpu as pltpu
from jax.sharding import PartitionSpec as P

ROPE_THETA = 500000.0
NORM_EPS = 1e-6
F32 = jnp.float32
BF16 = jnp.bfloat16


def rms_factor(sq_sum, full_width):
    return lax.rsqrt(sq_sum / full_width + NORM_EPS)


def tail_kernel(dims, o_ref, ga_ref, gm_ref, x_hbm, wo_hbm, w1_hbm, w3_hbm, w2_hbm, y_hbm,
                buf, r0, r1, r2, st, own, act, gains, w1, w3, w2,
                send_sem, recv_sem, w_sem, o_sem, x_sem, y_sem, free_sem):
    n_chunks, rows, d_model, q_loc, ff_loc = dims
    blk = rows // 8
    half_d = d_model // 2
    tp = lax.axis_index('tp')
    core = lax.rem(tp, 2)
    xb = lax.rem(lax.div(tp, 2), 2)
    yb = lax.div(tp, 4)
    sib = tp + 1 - 2 * core
    x_nb = tp + 2 - 4 * xb
    y_nb = tp + 4 - 8 * yb
    oc, ox, oy = 1 - core, 1 - xb, 1 - yb
    cols = (pl.ds(0, half_d), pl.ds(half_d, half_d))
    me = core * 4 + xb * 2 + yb

    n_wo = 4
    wo_tile = d_model // n_wo

    def wo_copy(j):
        cs = pl.ds(j * wo_tile, wo_tile)
        return pltpu.make_async_copy(wo_hbm.at[:, cs], w2.at[pl.ds(0, q_loc), cs], o_sem.at[j])

    def x_copy():
        return pltpu.make_async_copy(x_hbm.at[:, me], own, x_sem)

    n_k = 4
    k_rows = ff_loc // n_k

    def w_copy(i, j):
        src, dst = ((w1_hbm, w1), (w3_hbm, w3), (w2_hbm, w2))[i]
        rs = pl.ds(j * k_rows, k_rows)
        return pltpu.make_async_copy(src.at[rs], dst.at[rs], w_sem.at[i, j])

    for j in range(n_wo):
        wo_copy(j).start()
    x_copy().start()
    for j in range(n_k):
        for i in range(2):
            w_copy(i, j).start()

    barrier = pltpu.get_barrier_semaphore()
    for peer in (sib, x_nb, y_nb):
        pl.semaphore_signal(barrier, inc=1, device_id={'tp': peer}, device_id_type=pl.DeviceIdType.MESH)
    for i, g_ref in enumerate((ga_ref, gm_ref)):
        for j in range(d_model // 128):
            gains[i:i + 1, j * 128:(j + 1) * 128] = g_ref[j:j + 1, :].astype(F32)
    pl.semaphore_wait(barrier, 3)

    def xfer(k, c, s):
        ab = s % 2
        cs = cols[ab]
        b = buf.at[c]
        if s < 2:
            src, dst, peer = b.at[oc, :, :, :, cs], r0.at[c, :, :, :, cs], sib
        elif s == 2:
            src, dst, peer = b.at[core, ox, :, :, cs], r1.at[c, :, :, cs], x_nb
        elif s == 3:
            src, dst, peer = b.at[core, :, oy, :, cs], r1.at[c, :, :, cs], y_nb
        elif s < 6:
            src, dst, peer = st.at[c, :, cs], r2.at[c, :, cs], (y_nb, x_nb)[ab]
        else:
            if s < 8:
                src, peer = b.at[core, xb, yb, :, cs], (y_nb, x_nb)[ab]
            elif s == 8:
                src, peer = b.at[core, xb, :, :, cs], x_nb
            elif s == 9:
                src, peer = b.at[core, :, yb, :, cs], y_nb
            else:
                src, peer = b.at[core, :, :, :, cs], sib
            dst = src
        return pltpu.make_async_remote_copy(
            src_ref=src, dst_ref=dst, send_sem=send_sem.at[k, c, s], recv_sem=recv_sem.at[k, c, s],
            device_id={'tp': peer}, device_id_type=pl.DeviceIdType.MESH)

    def start(k, c, s):
        xfer(k, c, s).start()

    def s0(k, c, ab):
        start(k, c, ab)

    def s1(k, c, ab):
        cs = cols[ab]
        x = xfer(k, c, ab)
        x.wait_recv()
        if ab == 0:
            buf[c, core, ox, :, :, cs] = buf[c, core, ox, :, :, cs] + r0[c, ox, :, :, cs]
            start(k, c, 2)
            buf[c, core, xb, :, :, cs] = buf[c, core, xb, :, :, cs] + r0[c, xb, :, :, cs]
        else:
            for i in range(2):
                buf[c, core, i, oy, :, cs] = buf[c, core, i, oy, :, cs] + r0[c, i, oy, :, cs]
            start(k, c, 3)
            for i in range(2):
                buf[c, core, i, yb, :, cs] = buf[c, core, i, yb, :, cs] + r0[c, i, yb, :, cs]
        x.wait_send()
        if ab == 1:
            pl.semaphore_signal(free_sem.at[k, c], inc=1, device_id={'tp': sib}, device_id_type=pl.DeviceIdType.MESH)

    def s2(k, c, ab):
        cs = cols[ab]
        x = xfer(k, c, 2 + ab)
        x.wait_recv()
        if ab == 0:
            st[c, :, cs] = buf[c, core, xb, oy, :, cs] + r1[c, oy, :, cs]
            start(k, c, 4)
            buf[c, core, xb, yb, :, cs] = buf[c, core, xb, yb, :, cs] + r1[c, yb, :, cs]
        else:
            st[c, :, cs] = buf[c, core, ox, yb, :, cs] + r1[c, ox, :, cs]
            start(k, c, 5)
            buf[c, core, xb, yb, :, cs] = buf[c, core, xb, yb, :, cs] + r1[c, xb, :, cs]
        x.wait_send()

    v_tile = 512

    def s3(k, c):
        xfer(k, c, 4).wait_recv()
        xfer(k, c, 5).wait_recv()
        sq = jnp.zeros((blk, v_tile), F32)
        for j in range(d_model // v_tile):
            cs = pl.ds(j * v_tile, v_tile)
            tot = (buf[c, core, xb, yb, :, cs].astype(F32) + r2[c, :, cs].astype(F32)).astype(BF16)
            buf[c, core, xb, yb, :, cs] = tot
            tot = tot.astype(F32)
            sq = sq + tot * tot
        scale = rms_factor(jnp.sum(sq, axis=-1, keepdims=True), d_model)
        for ab in range(2):
            for j in range(half_d // v_tile):
                cs = pl.ds(ab * half_d + j * v_tile, v_tile)
                res = (own[c, :, cs].astype(F32) + buf[c, core, xb, yb, :, cs].astype(F32) * scale * gains[k:k + 1, cs]).astype(BF16)
                buf[c, core, xb, yb, :, cs] = res
                if k == 0:
                    own[c, :, cs] = res
            start(k, c, 6 + ab)
        xfer(k, c, 4).wait_send()
        xfer(k, c, 5).wait_send()

    def g2(k, c, ab):
        xfer(k, c, 6 + ab).wait_recv()
        start(k, c, 8 + ab)

    def g3(k, c, ab):
        xfer(k, c, 8 + ab).wait_recv()
        if ab == 0:
            pl.semaphore_wait(free_sem.at[k, c], 1)
        start(k, c, 10 + ab)

    def done(k, c):
        for s in (10, 11):
            xfer(k, c, s).wait_recv()
        for s in range(6, 12):
            xfer(k, c, s).wait_send()

    def y_copy(c):
        return pltpu.make_async_copy(buf.at[c], y_hbm.at[c], y_sem.at[c])

    def fin(k, c):
        done(k, c)
        y_copy(c).start()

    def both(fn, k, c):
        fn(k, c, 0)
        fn(k, c, 1)

    def p1(c):
        def body(j, carry):
            cs = pl.ds(pl.multiple_of(j * wo_tile, wo_tile), wo_tile)
            acc = jnp.dot(o_ref[c], w2[0:q_loc, cs], preferred_element_type=F32)
            buf[c, :, :, :, :, cs] = acc.astype(BF16).reshape(2, 2, 2, blk, wo_tile)
            return carry
        for ab in range(2):
            lax.fori_loop(ab * n_wo // 2, (ab + 1) * n_wo // 2, body, 0)
            s0(0, c, ab)

    gu_tile = 256
    gu_tiles = [(f, min(gu_tile, ff_loc - f)) for f in range(0, ff_loc, gu_tile)]

    def dot_t(w_rows, h):
        return lax.dot_general(w_rows, h, (((1,), (1,)), ((), ())), preferred_element_type=F32)

    def p2(services):
        def chunk(c, carry):
            def serve(point):
                for (sc, sp), fns in services.items():
                    if sp == point:
                        @pl.when(c == sc)
                        def _(fns=fns):
                            for fn in fns:
                                fn()

            for j, (f0, fw) in enumerate(gu_tiles):
                serve(j)
                h = buf[c].reshape(rows, d_model)
                g = dot_t(w1[f0:f0 + fw, :], h)
                up = dot_t(w3[f0:f0 + fw, :], h)
                act[:, f0:f0 + fw] = jnp.transpose(g * jax.nn.sigmoid(g) * up).astype(BF16)

            base = len(gu_tiles)

            def down(cs):
                acc = jnp.dot(act[...], w2[:, cs], preferred_element_type=F32)
                buf[c, :, :, :, :, cs] = acc.astype(BF16).reshape(2, 2, 2, blk, half_d)
            for ab in range(2):
                serve(base + ab)
                down(cols[ab])
                s0(1, c, ab)
            return carry
        lax.fori_loop(0, n_chunks, chunk, 0)

    for j in range(n_wo):
        wo_copy(j).wait()
    p1(0)
    p1(1)
    both(s1, 0, 0)
    p1(2)
    for j in range(n_k):
        w_copy(2, j).start()
    both(s1, 0, 1)
    both(s2, 0, 0)
    x_copy().wait()
    s3(0, 0)
    both(s2, 0, 1)
    both(g2, 0, 0)
    s3(0, 1)
    both(s1, 0, 2)
    both(g3, 0, 0)
    for j in range(n_k):
        for i in range(3):
            w_copy(i, j).wait()
    done(0, 0)

    F = functools.partial
    p2({
        (0, 0): [F(both, g2, 0, 1)],
        (0, 2): [F(both, s2, 0, 2)],
        (0, 5): [F(both, g3, 0, 1)],
        (0, 6): [F(s3, 0, 2)],
        (1, 0): [F(done, 0, 1), F(both, g2, 0, 2)],
        (1, 1): [F(both, s1, 1, 0)],
        (1, 4): [F(both, g3, 0, 2)],
        (1, 6): [F(both, s2, 1, 0)],
        (2, 0): [F(done, 0, 2), F(s3, 1, 0)],
        (2, 1): [F(both, s1, 1, 1)],
        (2, 3): [F(both, g2, 1, 0)],
        (2, 5): [F(both, s2, 1, 1)],
        (2, 7): [F(both, g3, 1, 0)],
    })
    s3(1, 1)
    fin(1, 0)
    both(s1, 1, 2)
    both(g2, 1, 1)
    both(s2, 1, 2)
    both(g3, 1, 1)
    s3(1, 2)
    fin(1, 1)
    both(g2, 1, 2)
    both(g3, 1, 2)
    fin(1, 2)
    for c in range(n_chunks):
        y_copy(c).wait()


def tail(o, x_seq, w_o, w1, w3, w2, g_attn, g_mlp):
    n_chunks, rows, d_model = x_seq.shape
    q_loc = o.shape[-1]
    ff_loc = w2.shape[0]
    blk = rows // 8
    dims = (n_chunks, rows, d_model, q_loc, ff_loc)
    vmem = pl.BlockSpec(memory_space=pltpu.VMEM)
    hbm = pl.BlockSpec(memory_space=pl.ANY)
    y = pl.pallas_call(
        functools.partial(tail_kernel, dims),
        name='tail',
        out_shape=jax.ShapeDtypeStruct((n_chunks, 2, 2, 2, blk, d_model), BF16),
        in_specs=[vmem, vmem, vmem, hbm, hbm, hbm, hbm, hbm],
        out_specs=hbm,
        scratch_shapes=[
            pltpu.VMEM((n_chunks, 2, 2, 2, blk, d_model), BF16),
            pltpu.VMEM((n_chunks, 2, 2, blk, d_model), BF16),
            pltpu.VMEM((n_chunks, 2, blk, d_model), BF16),
            pltpu.VMEM((n_chunks, blk, d_model), BF16),
            pltpu.VMEM((n_chunks, blk, d_model), BF16),
            pltpu.VMEM((n_chunks, blk, d_model), BF16),
            pltpu.VMEM((rows, ff_loc), BF16),
            pltpu.VMEM((2, d_model), F32),
            pltpu.VMEM((ff_loc, d_model), BF16),
            pltpu.VMEM((ff_loc, d_model), BF16),
            pltpu.VMEM((ff_loc, d_model), BF16),
            pltpu.SemaphoreType.DMA((2, n_chunks, 12)),
            pltpu.SemaphoreType.DMA((2, n_chunks, 12)),
            pltpu.SemaphoreType.DMA((3, 4)),
            pltpu.SemaphoreType.DMA((4,)),
            pltpu.SemaphoreType.DMA,
            pltpu.SemaphoreType.DMA((n_chunks,)),
            pltpu.SemaphoreType.REGULAR((2, n_chunks)),
        ],
        compiler_params=pltpu.CompilerParams(collective_id=1, has_side_effects=True, vmem_limit_bytes=67043328),
    )(o, g_attn.reshape(-1, 128), g_mlp.reshape(-1, 128), x_seq.reshape(n_chunks, 8, blk, d_model), w_o, w1.T, w3.T, w2)
    return y.reshape(n_chunks, rows, d_model)


def head_kernel(dims, len_ref, gq_ref, gk_ref, freq_ref, x_hbm, wq_hbm, wk_hbm, wv_hbm, q_out, k_out, v_out,
                x, w, raw, cos_t, sin_t, sums, x_sem, w_sem, send_sem, recv_sem):
    n_steps, rows, d_model, q_loc, hd, n_tp = dims
    heads = q_loc // hd
    width = q_loc + 2 * hd
    tp = lax.axis_index('tp')

    def x_copy(t):
        return pltpu.make_async_copy(x_hbm.at[t], x.at[t], x_sem.at[t])

    n_k = 4
    k_rows = d_model // n_k

    def w_copies(j):
        rs = pl.ds(j * k_rows, k_rows)
        return (pltpu.make_async_copy(wq_hbm.at[rs], w.at[rs, pl.ds(0, q_loc)], w_sem.at[0, j]),
                pltpu.make_async_copy(wk_hbm.at[rs], w.at[rs, pl.ds(q_loc, hd)], w_sem.at[1, j]),
                pltpu.make_async_copy(wv_hbm.at[rs], w.at[rs, pl.ds(q_loc + hd, hd)], w_sem.at[2, j]))

    x_copy(0).start()
    for j in range(n_k):
        for cp in w_copies(j):
            cp.start()
    for t in range(1, n_steps):
        x_copy(t).start()

    barrier = pltpu.get_barrier_semaphore()
    peers = [lax.rem(tp + d, n_tp) for d in range(1, n_tp)]
    for p in peers:
        pl.semaphore_signal(barrier, inc=1, device_id={'tp': p}, device_id_type=pl.DeviceIdType.MESH)

    lens = jnp.transpose(jnp.broadcast_to(len_ref[...].astype(F32), (rows, rows)))
    lane = lax.broadcasted_iota(jnp.int32, (rows, hd), 1)
    sign = jnp.where(lane < hd // 2, -1.0, 1.0).astype(F32)
    for t in range(n_steps):
        ang = (lens + float(t)) * freq_ref[...]
        cos_t[t] = jnp.cos(ang)
        sin_t[t] = jnp.sin(ang) * sign

    for j in range(n_k):
        for cp in w_copies(j):
            cp.wait()
    part = jnp.zeros((rows, rows), F32)
    sq_lane = lax.broadcasted_iota(jnp.int32, (rows, rows), 1)
    for t in range(n_steps):
        x_copy(t).wait()
        res = jnp.dot(x[t], w[...], preferred_element_type=F32).astype(BF16)
        raw[t] = res
        q = res[:, :q_loc].astype(F32)
        k = res[:, q_loc:q_loc + hd].astype(F32)
        part = jnp.where(sq_lane == 2 * t, jnp.sum(q * q, axis=-1, keepdims=True), part)
        part = jnp.where(sq_lane == 2 * t + 1, jnp.sum(k * k, axis=-1, keepdims=True), part)
    sums[tp] = jnp.transpose(part)[0:8]
    pl.semaphore_wait(barrier, n_tp - 1)

    def send(d):
        return pltpu.make_async_remote_copy(
            src_ref=sums.at[tp], dst_ref=sums.at[tp], send_sem=send_sem.at[d], recv_sem=recv_sem.at[d],
            device_id={'tp': peers[d]}, device_id_type=pl.DeviceIdType.MESH)

    for d in range(n_tp - 1):
        send(d).start()
    q_out[pl.ds(n_steps * heads, rows, stride=16), :] = jnp.zeros((rows, hd), F32)
    for t in range(n_steps):
        v_out[t] = raw[t, :, q_loc + hd:width].astype(F32)
    for d in range(n_tp - 1):
        send(d).wait()
    tot = sums[0]
    for d in range(1, n_tp):
        tot = tot + sums[d]
    full = jnp.transpose(jnp.concatenate([tot, jnp.zeros((rows - 8, rows), F32)], axis=0))
    for t in range(n_steps):
        q_scale = rms_factor(full[:, 2 * t:2 * t + 1], q_loc * n_tp)
        k_scale = rms_factor(full[:, 2 * t + 1:2 * t + 2], hd * n_tp)

        def rotate(col, scale, gain):
            val = raw[t, :, col:col + hd].astype(F32) * scale * gain.astype(F32)
            return (val * cos_t[t] + pltpu.roll(val, hd // 2, 1) * sin_t[t]).astype(BF16).astype(F32)
        for j in range(heads):
            q_out[pl.ds(t * heads + j, rows, stride=16), :] = rotate(j * hd, q_scale, gq_ref[j:j + 1, :])
        k_out[t] = rotate(q_loc, k_scale, gk_ref[...])


def head(x_seq, cache_len, w_q, w_k, w_v, g_q, g_k, n_tp):
    n_steps, rows, d_model = x_seq.shape
    q_loc, hd = w_q.shape[1], w_k.shape[1]
    width = q_loc + 2 * hd
    half = hd // 2
    inv_freq = np.float32(ROPE_THETA) ** (-(np.arange(half, dtype=np.float32) * np.float32(2.0 / hd)))
    freq = jnp.asarray(np.concatenate([inv_freq, inv_freq]).reshape(1, hd), F32)
    vmem = pl.BlockSpec(memory_space=pltpu.VMEM)
    hbm = pl.BlockSpec(memory_space=pl.ANY)
    return pl.pallas_call(
        functools.partial(head_kernel, (n_steps, rows, d_model, q_loc, hd, n_tp)),
        name='head',
        out_shape=(jax.ShapeDtypeStruct((rows * 16, hd), F32),
                   jax.ShapeDtypeStruct((n_steps, rows, hd), F32),
                   jax.ShapeDtypeStruct((n_steps, rows, hd), F32)),
        in_specs=[vmem] * 4 + [hbm] * 4,
        out_specs=(vmem,) * 3,
        scratch_shapes=[
            pltpu.VMEM((n_steps, rows, d_model), BF16),
            pltpu.VMEM((d_model, width), BF16),
            pltpu.VMEM((n_steps, rows, width), BF16),
            pltpu.VMEM((n_steps, rows, hd), F32),
            pltpu.VMEM((n_steps, rows, hd), F32),
            pltpu.VMEM((n_tp, 8, rows), F32),
            pltpu.SemaphoreType.DMA((n_steps,)),
            pltpu.SemaphoreType.DMA((3, 4)),
            pltpu.SemaphoreType.DMA((n_tp - 1,)),
            pltpu.SemaphoreType.DMA((n_tp - 1,)),
        ],
        compiler_params=pltpu.CompilerParams(collective_id=0, has_side_effects=True, vmem_limit_bytes=67043328),
    )(cache_len.reshape(1, -1), g_q.reshape(-1, hd), g_k.reshape(1, -1), freq, x_seq, w_q, w_k, w_v)


def attn_kernel(dims, len_ref, q_ref, kn_ref, vn_ref, k_ref, v_ref, o_ref, ko_ref, vo_ref, s_scr, e_scr, l_scr, o_scr):
    n_steps, nb, heads, hd, seq_max = dims
    first = pl.program_id(0) * nb
    win = 32
    row_step = lax.broadcasted_iota(jnp.int32, (16, seq_max), 0) // heads
    col = lax.broadcasted_iota(jnp.int32, (16, seq_max), 1)
    ahead = col - row_step
    win_row = lax.broadcasted_iota(jnp.int32, (win, hd), 0)
    for src, new, dst in ((k_ref, kn_ref, ko_ref), (v_ref, vn_ref, vo_ref)):
        dst[...] = src[...]
        for i in range(nb):
            ln = len_ref[first + i]
            base = pl.multiple_of(jnp.minimum((ln // 16) * 16, seq_max - win), 16)
            rel = win_row + (base - ln)
            cut = src[i, pl.ds(base, win), :].astype(F32)
            for t in range(n_steps):
                cut = jnp.where(rel == t, new[t, i:i + 1, :], cut)
            dst[i, pl.ds(base, win), :] = cut.astype(BF16)
    for i in range(nb):
        s = lax.dot_general(q_ref[i].astype(BF16), ko_ref[i], (((1,), (1,)), ((), ())), preferred_element_type=F32) * hd ** -0.5
        s_scr[i * 16:(i + 1) * 16, :] = jnp.where(ahead <= len_ref[first + i], s, -jnp.inf)
    for i in range(0, nb, 2):
        rs = slice(i * 16, (i + 2) * 16)
        s = s_scr[rs, :]
        e = jnp.exp(s - jnp.max(s, axis=-1, keepdims=True))
        l_scr[rs, :] = jnp.broadcast_to(jnp.sum(e, axis=-1, keepdims=True), (32, hd))
        e_scr[rs, :] = e.astype(BF16)
    for i in range(nb):
        rs = slice(i * 16, (i + 1) * 16)
        o_scr[rs, :] = jnp.dot(e_scr[rs, :], vo_ref[i], preferred_element_type=F32)
    o_scr[...] = o_scr[...] / l_scr[...]
    for t in range(n_steps):
        for j in range(heads):
            o_ref[t, :, j * hd:(j + 1) * hd] = o_scr[pl.ds(t * heads + j, nb, stride=16), :].astype(BF16)


def attend(q, kn, vn, k_cache, v_cache, cache_len, heads):
    n_rows, _, seq_max, hd = k_cache.shape
    n_steps = kn.shape[0]
    nb = 32
    cache_spec = pl.BlockSpec((nb, seq_max, hd), lambda i, ln: (i, 0, 0))
    new_spec = pl.BlockSpec((n_steps, nb, hd), lambda i, ln: (0, i, 0))
    cache_shape = jax.ShapeDtypeStruct((n_rows, seq_max, hd), BF16)
    flops = 4 * n_rows * 16 * seq_max * hd
    return pl.pallas_call(
        functools.partial(attn_kernel, (n_steps, nb, heads, hd, seq_max)),
        name='attend',
        grid_spec=pltpu.PrefetchScalarGridSpec(
            num_scalar_prefetch=1,
            grid=(n_rows // nb,),
            in_specs=[pl.BlockSpec((nb, 16, hd), lambda i, ln: (i, 0, 0)), new_spec, new_spec, cache_spec, cache_spec],
            out_specs=(pl.BlockSpec((n_steps, nb, heads * hd), lambda i, ln: (0, i, 0)), cache_spec, cache_spec),
            scratch_shapes=[pltpu.VMEM((nb * 16, seq_max), F32), pltpu.VMEM((nb * 16, seq_max), BF16), pltpu.VMEM((nb * 16, hd), F32), pltpu.VMEM((nb * 16, hd), F32)],
        ),
        out_shape=(jax.ShapeDtypeStruct((n_steps, n_rows, heads * hd), BF16), cache_shape, cache_shape),
        compiler_params=pltpu.CompilerParams(vmem_limit_bytes=67043328),
        cost_estimate=pl.CostEstimate(flops=flops, bytes_accessed=4 * n_rows * seq_max * hd * 2, transcendentals=n_rows * 16 * seq_max),
    )(cache_len, q.reshape(n_rows, 16, hd), kn, vn, k_cache[:, 0], v_cache[:, 0])


def local_layer(n_tp, x_seq, cache_len, k_cache, v_cache, w_q, w_k, w_v, w_o, w_gate, w_up, w_down, g_q, g_k, g_attn, g_mlp):
    heads = w_q.shape[1] // k_cache.shape[3]
    q, kn, vn = head(x_seq, cache_len, w_q, w_k, w_v, g_q, g_k, n_tp)
    o, k_out, v_out = attend(q, kn, vn, k_cache, v_cache, cache_len, heads)
    y = tail(o, x_seq, w_o, w_gate, w_up, w_down, g_attn, g_mlp)
    return y, k_out[:, None], v_out[:, None]


def solution(mesh):
    tp_size = mesh.shape['tp']
    data_spec = P(None, 'dp', None)
    cache_spec = P('dp', 'tp', None, None)
    col_spec = P(None, 'tp')
    row_spec = P('tp', None)
    arg_specs = (data_spec, P('dp'), cache_spec, cache_spec, col_spec, col_spec, col_spec, row_spec, col_spec, col_spec, row_spec, P('tp'), P('tp'), P(None), P(None))
    out_specs = (data_spec, cache_spec, cache_spec)
    return jax.shard_map(functools.partial(local_layer, tp_size), mesh=mesh, in_specs=arg_specs, out_specs=out_specs, check_vma=False)
```

time: 204 us -> 145 us (0.71)
  Pallas kernels: 194 us -> 140 us
  local copies, waits for them, and re-layouts: 8.17 us -> 4.29 us
    pallas_call x1, Pallas kernels: 140 us -> 106 us  [tail(): pl.pallas_call(functools.partial(tail_kernel, dims), name='tail', out_sha...]
    pallas_call x1, Pallas kernels: 35.7 us -> 15.2 us  [attend(): pl.pallas_call(functools.partial(attn_kernel, (n_steps, nb, heads, hd, se...]
    reshape x3 -> x0, local copies, waits for them, and re-layouts: 3.88 us -> none  [the longest x1 1.31 us: tail(): g_mlp.reshape(1, -1)]
where the time goes in v3:
time: 145 us
  Pallas kernels  140 us (97%)
  local copies, waits for them, and re-layouts  4.29 us (3%)
    pallas_call x1, Pallas kernels, tail(): pl.pallas_call(functools.partial(tail_kernel, dims), name='tail', out_sha...  106 us
    pallas_call x1, Pallas kernels, head(): pl.pallas_call(functools.partial(head_kernel, (n_steps, rows, d_model, q_...  18.4 us
    pallas_call x1, Pallas kernels, attend(): pl.pallas_call(functools.partial(attn_kernel, (n_steps, nb, heads, hd, se...  15.2 us
    unnamed x1, local copies, waits for them, and re-layouts  4.29 us

profile of v3, /device:TPU:0, one launch (start us, length us, event | category | flops | bytes accessed | tf_op | source)
XLA Modules:
  0.0 144.9 jit_solution(5616261285982751255)
XLA Ops:
  0.6 18.4 %head.1 = (f32[2048,128]{1,0:T(8,128)}, f32[3,128,128]{2,1,0:T(8,128)}, f32[3,128,128]{2,1,0:T(8,128)}) custom-call(s32[1,128]{1,0:T(1,128)} %bitcast.28, bf16[5,128]{1,0:T(8,128)(2,1)} %bitcast.27, bf16[1,128]{1,0:T(2,128)(2,1)} %bitcast.29, f32[1,128]{1,0:T(1,128)} %constant.2.clone.freq_ref, bf16[3,128,5120]{2,1,0:T(8,128)(2,1)} %x_hbm.1, ...), custom_call_target="tpu_custom_call" | custom-call | tf_op jit(solution)/shard_map/head/pallas_call | solution.py:415
  19.0 15.2 %attend.1 = (bf16[3,128,640]{2,1,0:T(8,128)(2,1)}, bf16[128,256,128]{2,1,0:T(8,128)(2,1)}, bf16[128,256,128]{2,1,0:T(8,128)(2,1)}) custom-call(s32[128]{0:T(128)} %len_ref.1, f32[128,16,128]{2,1,0:T(8,128)} %bitcast.24, f32[3,128,128]{2,1,0:T(8,128)} %get-tuple-element.10.kn_ref, f32[3,128,128]{2,1,0:T(8,128)} %get-tuple-element.11.vn_ref, ...), custom_call_target="tpu_custom_call" | custom-call | flops 268435456 | bytes 33554432 | tf_op jit(solution)/shard_map/attend/pallas_call | solution.py:483
  34.2 106.4 %tail.1 = bf16[3,2,2,2,16,5120]{5,4,3,2,1,0:T(8,128)(2,1)} custom-call(bf16[3,128,640]{2,1,0:T(8,128)(2,1)} %get-tuple-element.12.o_ref, bf16[40,128]{1,0:T(8,128)(2,1)} %bitcast.25, bf16[40,128]{1,0:T(8,128)(2,1)} %bitcast.26, bf16[3,8,16,5120]{3,2,1,0:T(8,128)(2,1)} %bitcast.20, bf16[640,5120]{1,0:T(8,128)(2,1)} %wo_hbm.1, bf16[1728,5120]{1,0:T(8,128)(2,1)} %bitcast.18, ...), custom_call_target="tpu_custom_call" | custom-call | tf_op jit(solution)/shard_map/tail/pallas_call | solution.py:292
  140.6 4.3 %copy.22 = bf16[3,128,5120]{2,1,0:T(8,128)(2,1)} copy(bf16[3,128,5120]{2,1,0:T(8,128)(2,1)} %bitcast.21) | data formatting | bytes 7864320

commit v4 on v3

--- a/solution.py
+++ b/solution.py
@@ -56,9 +56,6 @@
     for j in range(n_wo):
         wo_copy(j).start()
     x_copy().start()
-    for j in range(n_k):
-        for i in range(2):
-            w_copy(i, j).start()
 
     barrier = pltpu.get_barrier_semaphore()
     for peer in (sib, x_nb, y_nb):
@@ -190,7 +187,12 @@
             buf[c, :, :, :, :, cs] = acc.astype(BF16).reshape(2, 2, 2, blk, wo_tile)
             return carry
         for ab in range(2):
-            lax.fori_loop(ab * n_wo // 2, (ab + 1) * n_wo // 2, body, 0)
+            if c == 0:
+                for j in range(ab * n_wo // 2, (ab + 1) * n_wo // 2):
+                    wo_copy(j).wait()
+                    body(j, 0)
+            else:
+                lax.fori_loop(ab * n_wo // 2, (ab + 1) * n_wo // 2, body, 0)
             s0(0, c, ab)
 
     gu_tile = 256
@@ -228,9 +230,10 @@
             return carry
         lax.fori_loop(0, n_chunks, chunk, 0)
 
-    for j in range(n_wo):
-        wo_copy(j).wait()
     p1(0)
+    for j in range(n_k):
+        for i in range(2):
+            w_copy(i, j).start()
     p1(1)
     both(s1, 0, 0)
     p1(2)
@@ -362,38 +365,36 @@
     for j in range(n_k):
         for cp in w_copies(j):
             cp.wait()
-    part = jnp.zeros((rows, rows), F32)
     sq_lane = lax.broadcasted_iota(jnp.int32, (rows, rows), 1)
-    for t in range(n_steps):
+
+    def send(t, d):
+        return pltpu.make_async_remote_copy(
+            src_ref=sums.at[t, tp], dst_ref=sums.at[t, tp], send_sem=send_sem.at[t, d], recv_sem=recv_sem.at[t, d],
+            device_id={'tp': peers[d]}, device_id_type=pl.DeviceIdType.MESH)
+
+    def project(t):
         x_copy(t).wait()
         res = jnp.dot(x[t], w[...], preferred_element_type=F32).astype(BF16)
         raw[t] = res
         q = res[:, :q_loc].astype(F32)
         k = res[:, q_loc:q_loc + hd].astype(F32)
-        part = jnp.where(sq_lane == 2 * t, jnp.sum(q * q, axis=-1, keepdims=True), part)
-        part = jnp.where(sq_lane == 2 * t + 1, jnp.sum(k * k, axis=-1, keepdims=True), part)
-    sums[tp] = jnp.transpose(part)[0:8]
-    pl.semaphore_wait(barrier, n_tp - 1)
-
-    def send(d):
-        return pltpu.make_async_remote_copy(
-            src_ref=sums.at[tp], dst_ref=sums.at[tp], send_sem=send_sem.at[d], recv_sem=recv_sem.at[d],
-            device_id={'tp': peers[d]}, device_id_type=pl.DeviceIdType.MESH)
-
-    for d in range(n_tp - 1):
-        send(d).start()
-    q_out[pl.ds(n_steps * heads, rows, stride=16), :] = jnp.zeros((rows, hd), F32)
-    for t in range(n_steps):
-        v_out[t] = raw[t, :, q_loc + hd:width].astype(F32)
-    for d in range(n_tp - 1):
-        send(d).wait()
-    tot = sums[0]
-    for d in range(1, n_tp):
-        tot = tot + sums[d]
-    full = jnp.transpose(jnp.concatenate([tot, jnp.zeros((rows - 8, rows), F32)], axis=0))
-    for t in range(n_steps):
-        q_scale = rms_factor(full[:, 2 * t:2 * t + 1], q_loc * n_tp)
-        k_scale = rms_factor(full[:, 2 * t + 1:2 * t + 2], hd * n_tp)
+        part = jnp.where(sq_lane == 0, jnp.sum(q * q, axis=-1, keepdims=True), jnp.sum(k * k, axis=-1, keepdims=True))
+        sums[t, tp] = jnp.transpose(part)[0:8]
+        if t == 0:
+            pl.semaphore_wait(barrier, n_tp - 1)
+        for d in range(n_tp - 1):
+            send(t, d).start()
+        v_out[t] = res[:, q_loc + hd:width].astype(F32)
+
+    def rotate_all(t):
+        for d in range(n_tp - 1):
+            send(t, d).wait()
+        tot = sums[t, 0]
+        for d in range(1, n_tp):
+            tot = tot + sums[t, d]
+        full = jnp.transpose(jnp.concatenate([tot, jnp.zeros((rows - 8, rows), F32)], axis=0))
+        q_scale = rms_factor(full[:, 0:1], q_loc * n_tp)
+        k_scale = rms_factor(full[:, 1:2], hd * n_tp)
 
         def rotate(col, scale, gain):
             val = raw[t, :, col:col + hd].astype(F32) * scale * gain.astype(F32)
@@ -401,6 +402,12 @@
         for j in range(heads):
             q_out[pl.ds(t * heads + j, rows, stride=16), :] = rotate(j * hd, q_scale, gq_ref[j:j + 1, :])
         k_out[t] = rotate(q_loc, k_scale, gk_ref[...])
+
+    for t in range(n_steps):
+        project(t)
+    q_out[pl.ds(n_steps * heads, rows, stride=16), :] = jnp.zeros((rows, hd), F32)
+    for t in range(n_steps):
+        rotate_all(t)
 
 
 def head(x_seq, cache_len, w_q, w_k, w_v, g_q, g_k, n_tp):
@@ -426,11 +433,11 @@
             pltpu.VMEM((n_steps, rows, width), BF16),
             pltpu.VMEM((n_steps, rows, hd), F32),
             pltpu.VMEM((n_steps, rows, hd), F32),
-            pltpu.VMEM((n_tp, 8, rows), F32),
+            pltpu.VMEM((n_steps, n_tp, 8, rows), F32),
             pltpu.SemaphoreType.DMA((n_steps,)),
             pltpu.SemaphoreType.DMA((3, 4)),
-            pltpu.SemaphoreType.DMA((n_tp - 1,)),
-            pltpu.SemaphoreType.DMA((n_tp - 1,)),
+            pltpu.SemaphoreType.DMA((n_steps, n_tp - 1)),
+            pltpu.SemaphoreType.DMA((n_steps, n_tp - 1)),
         ],
         compiler_params=pltpu.CompilerParams(collective_id=0, has_side_effects=True, vmem_limit_bytes=67043328),
     )(cache_len.reshape(1, -1), g_q.reshape(-1, hd), g_k.reshape(1, -1), freq, x_seq, w_q, w_k, w_v)

time: 145 us -> 135 us (0.931)
  Pallas kernels: 140 us -> 130 us
    pallas_call x1, Pallas kernels: 106 us -> 96.3 us  [tail(): pl.pallas_call(functools.partial(tail_kernel, dims), name='tail', out_sha...]
where the time goes in v4:
time: 135 us
  Pallas kernels  130 us (96%)
  local copies, waits for them, and re-layouts  4.29 us (3%)
    pallas_call x1, Pallas kernels, tail(): pl.pallas_call(functools.partial(tail_kernel, dims), name='tail', out_sha...  96.3 us
    pallas_call x1, Pallas kernels, head(): pl.pallas_call(functools.partial(head_kernel, (n_steps, rows, d_model, q_...  18.1 us
    pallas_call x1, Pallas kernels, attend(): pl.pallas_call(functools.partial(attn_kernel, (n_steps, nb, heads, hd, se...  15.2 us
    unnamed x1, local copies, waits for them, and re-layouts  4.29 us

profile of v4, /device:TPU:0, one launch (start us, length us, event | category | flops | bytes accessed | tf_op | source)
XLA Modules:
  0.0 134.6 jit_solution(9684352494257940006)
XLA Ops:
  0.6 18.1 %head.1 = (f32[2048,128]{1,0:T(8,128)}, f32[3,128,128]{2,1,0:T(8,128)}, f32[3,128,128]{2,1,0:T(8,128)}) custom-call(s32[1,128]{1,0:T(1,128)} %bitcast.28, bf16[5,128]{1,0:T(8,128)(2,1)} %bitcast.27, bf16[1,128]{1,0:T(2,128)(2,1)} %bitcast.29, f32[1,128]{1,0:T(1,128)} %constant.2.clone.freq_ref, bf16[3,128,5120]{2,1,0:T(8,128)(2,1)} %x_hbm.1, ...), custom_call_target="tpu_custom_call" | custom-call | tf_op jit(solution)/shard_map/head/pallas_call | solution.py:422
  18.8 15.2 %attend.1 = (bf16[3,128,640]{2,1,0:T(8,128)(2,1)}, bf16[128,256,128]{2,1,0:T(8,128)(2,1)}, bf16[128,256,128]{2,1,0:T(8,128)(2,1)}) custom-call(s32[128]{0:T(128)} %len_ref.1, f32[128,16,128]{2,1,0:T(8,128)} %bitcast.24, f32[3,128,128]{2,1,0:T(8,128)} %get-tuple-element.10.kn_ref, f32[3,128,128]{2,1,0:T(8,128)} %get-tuple-element.11.vn_ref, ...), custom_call_target="tpu_custom_call" | custom-call | flops 268435456 | bytes 33554432 | tf_op jit(solution)/shard_map/attend/pallas_call | solution.py:490
  34.0 96.3 %tail.1 = bf16[3,2,2,2,16,5120]{5,4,3,2,1,0:T(8,128)(2,1)} custom-call(bf16[3,128,640]{2,1,0:T(8,128)(2,1)} %get-tuple-element.12.o_ref, bf16[40,128]{1,0:T(8,128)(2,1)} %bitcast.25, bf16[40,128]{1,0:T(8,128)(2,1)} %bitcast.26, bf16[3,8,16,5120]{3,2,1,0:T(8,128)(2,1)} %bitcast.20, bf16[640,5120]{1,0:T(8,128)(2,1)} %wo_hbm.1, bf16[1728,5120]{1,0:T(8,128)(2,1)} %bitcast.18, ...), custom_call_target="tpu_custom_call" | custom-call | tf_op jit(solution)/shard_map/tail/pallas_call | solution.py:295
  130.3 4.3 %copy.22 = bf16[3,128,5120]{2,1,0:T(8,128)(2,1)} copy(bf16[3,128,5120]{2,1,0:T(8,128)(2,1)} %bitcast.21) | data formatting | bytes 7864320

commit v5 on v4

--- a/solution.py
+++ b/solution.py
@@ -32,7 +32,9 @@
     x_nb = tp + 2 - 4 * xb
     y_nb = tp + 4 - 8 * yb
     oc, ox, oy = 1 - core, 1 - xb, 1 - yb
-    cols = (pl.ds(0, half_d), pl.ds(half_d, half_d))
+    n_p = 4
+    wide = d_model // n_p
+    cols = [pl.ds(p * wide, wide) for p in range(n_p)]
     me = core * 4 + xb * 2 + yb
 
     n_wo = 4
@@ -65,109 +67,105 @@
             gains[i:i + 1, j * 128:(j + 1) * 128] = g_ref[j:j + 1, :].astype(F32)
     pl.semaphore_wait(barrier, 3)
 
-    def xfer(k, c, s):
-        ab = s % 2
-        cs = cols[ab]
+    def xfer(k, c, ph, p):
+        odd = p % 2
+        cs = cols[p]
         b = buf.at[c]
-        if s < 2:
+        if ph == 0:
             src, dst, peer = b.at[oc, :, :, :, cs], r0.at[c, :, :, :, cs], sib
-        elif s == 2:
-            src, dst, peer = b.at[core, ox, :, :, cs], r1.at[c, :, :, cs], x_nb
-        elif s == 3:
-            src, dst, peer = b.at[core, :, oy, :, cs], r1.at[c, :, :, cs], y_nb
-        elif s < 6:
-            src, dst, peer = st.at[c, :, cs], r2.at[c, :, cs], (y_nb, x_nb)[ab]
+        elif ph == 1:
+            src = b.at[core, :, oy, :, cs] if odd else b.at[core, ox, :, :, cs]
+            dst, peer = r1.at[c, :, :, cs], (x_nb, y_nb)[odd]
+        elif ph == 2:
+            src, dst, peer = st.at[c, :, cs], r2.at[c, :, cs], (y_nb, x_nb)[odd]
         else:
-            if s < 8:
-                src, peer = b.at[core, xb, yb, :, cs], (y_nb, x_nb)[ab]
-            elif s == 8:
-                src, peer = b.at[core, xb, :, :, cs], x_nb
-            elif s == 9:
-                src, peer = b.at[core, :, yb, :, cs], y_nb
+            if ph == 3:
+                src, peer = b.at[core, xb, yb, :, cs], (y_nb, x_nb)[odd]
+            elif ph == 4:
+                src = b.at[core, :, yb, :, cs] if odd else b.at[core, xb, :, :, cs]
+                peer = (x_nb, y_nb)[odd]
             else:
                 src, peer = b.at[core, :, :, :, cs], sib
             dst = src
         return pltpu.make_async_remote_copy(
-            src_ref=src, dst_ref=dst, send_sem=send_sem.at[k, c, s], recv_sem=recv_sem.at[k, c, s],
+            src_ref=src, dst_ref=dst, send_sem=send_sem.at[k, c, ph * n_p + p], recv_sem=recv_sem.at[k, c, ph * n_p + p],
             device_id={'tp': peer}, device_id_type=pl.DeviceIdType.MESH)
 
-    def start(k, c, s):
-        xfer(k, c, s).start()
-
-    def s0(k, c, ab):
-        start(k, c, ab)
-
-    def s1(k, c, ab):
-        cs = cols[ab]
-        x = xfer(k, c, ab)
+    def start(k, c, ph, p):
+        xfer(k, c, ph, p).start()
+
+    def s1(k, c, p):
+        cs = cols[p]
+        x = xfer(k, c, 0, p)
         x.wait_recv()
-        if ab == 0:
+        if p % 2 == 0:
             buf[c, core, ox, :, :, cs] = buf[c, core, ox, :, :, cs] + r0[c, ox, :, :, cs]
-            start(k, c, 2)
+            start(k, c, 1, p)
             buf[c, core, xb, :, :, cs] = buf[c, core, xb, :, :, cs] + r0[c, xb, :, :, cs]
         else:
             for i in range(2):
                 buf[c, core, i, oy, :, cs] = buf[c, core, i, oy, :, cs] + r0[c, i, oy, :, cs]
-            start(k, c, 3)
+            start(k, c, 1, p)
             for i in range(2):
                 buf[c, core, i, yb, :, cs] = buf[c, core, i, yb, :, cs] + r0[c, i, yb, :, cs]
         x.wait_send()
-        if ab == 1:
+        if p == n_p - 1:
             pl.semaphore_signal(free_sem.at[k, c], inc=1, device_id={'tp': sib}, device_id_type=pl.DeviceIdType.MESH)
 
-    def s2(k, c, ab):
-        cs = cols[ab]
-        x = xfer(k, c, 2 + ab)
+    def s2(k, c, p):
+        cs = cols[p]
+        x = xfer(k, c, 1, p)
         x.wait_recv()
-        if ab == 0:
+        if p % 2 == 0:
             st[c, :, cs] = buf[c, core, xb, oy, :, cs] + r1[c, oy, :, cs]
-            start(k, c, 4)
+            start(k, c, 2, p)
             buf[c, core, xb, yb, :, cs] = buf[c, core, xb, yb, :, cs] + r1[c, yb, :, cs]
         else:
             st[c, :, cs] = buf[c, core, ox, yb, :, cs] + r1[c, ox, :, cs]
-            start(k, c, 5)
+            start(k, c, 2, p)
             buf[c, core, xb, yb, :, cs] = buf[c, core, xb, yb, :, cs] + r1[c, xb, :, cs]
         x.wait_send()
 
-    v_tile = 512
+    v_tile = 256
 
     def s3(k, c):
-        xfer(k, c, 4).wait_recv()
-        xfer(k, c, 5).wait_recv()
         sq = jnp.zeros((blk, v_tile), F32)
         for j in range(d_model // v_tile):
+            if j * v_tile % wide == 0:
+                xfer(k, c, 2, j * v_tile // wide).wait_recv()
             cs = pl.ds(j * v_tile, v_tile)
             tot = (buf[c, core, xb, yb, :, cs].astype(F32) + r2[c, :, cs].astype(F32)).astype(BF16)
             buf[c, core, xb, yb, :, cs] = tot
             tot = tot.astype(F32)
             sq = sq + tot * tot
         scale = rms_factor(jnp.sum(sq, axis=-1, keepdims=True), d_model)
-        for ab in range(2):
-            for j in range(half_d // v_tile):
-                cs = pl.ds(ab * half_d + j * v_tile, v_tile)
+        for p in range(n_p):
+            for j in range(wide // v_tile):
+                cs = pl.ds(p * wide + j * v_tile, v_tile)
                 res = (own[c, :, cs].astype(F32) + buf[c, core, xb, yb, :, cs].astype(F32) * scale * gains[k:k + 1, cs]).astype(BF16)
                 buf[c, core, xb, yb, :, cs] = res
                 if k == 0:
                     own[c, :, cs] = res
-            start(k, c, 6 + ab)
-        xfer(k, c, 4).wait_send()
-        xfer(k, c, 5).wait_send()
-
-    def g2(k, c, ab):
-        xfer(k, c, 6 + ab).wait_recv()
-        start(k, c, 8 + ab)
-
-    def g3(k, c, ab):
-        xfer(k, c, 8 + ab).wait_recv()
-        if ab == 0:
+            start(k, c, 3, p)
+        for p in range(n_p):
+            xfer(k, c, 2, p).wait_send()
+
+    def g2(k, c, p):
+        xfer(k, c, 3, p).wait_recv()
+        start(k, c, 4, p)
+
+    def g3(k, c, p):
+        xfer(k, c, 4, p).wait_recv()
+        if p == 0:
             pl.semaphore_wait(free_sem.at[k, c], 1)
-        start(k, c, 10 + ab)
+        start(k, c, 5, p)
 
     def done(k, c):
-        for s in (10, 11):
-            xfer(k, c, s).wait_recv()
-        for s in range(6, 12):
-            xfer(k, c, s).wait_send()
+        for p in range(n_p):
+            xfer(k, c, 5, p).wait_recv()
+        for ph in range(3, 6):
+            for p in range(n_p):
+                xfer(k, c, ph, p).wait_send()
 
     def y_copy(c):
         return pltpu.make_async_copy(buf.at[c], y_hbm.at[c], y_sem.at[c])
@@ -177,23 +175,16 @@
         y_copy(c).start()
 
     def both(fn, k, c):
-        fn(k, c, 0)
-        fn(k, c, 1)
+        for p in range(n_p):
+            fn(k, c, p)
 
     def p1(c):
-        def body(j, carry):
-            cs = pl.ds(pl.multiple_of(j * wo_tile, wo_tile), wo_tile)
-            acc = jnp.dot(o_ref[c], w2[0:q_loc, cs], preferred_element_type=F32)
-            buf[c, :, :, :, :, cs] = acc.astype(BF16).reshape(2, 2, 2, blk, wo_tile)
-            return carry
-        for ab in range(2):
+        for p in range(n_p):
             if c == 0:
-                for j in range(ab * n_wo // 2, (ab + 1) * n_wo // 2):
-                    wo_copy(j).wait()
-                    body(j, 0)
-            else:
-                lax.fori_loop(ab * n_wo // 2, (ab + 1) * n_wo // 2, body, 0)
-            s0(0, c, ab)
+                wo_copy(p).wait()
+            acc = jnp.dot(o_ref[c], w2[0:q_loc, cols[p]], preferred_element_type=F32)
+            buf[c, :, :, :, :, cols[p]] = acc.astype(BF16).reshape(2, 2, 2, blk, wide)
+            start(0, c, 0, p)
 
     gu_tile = 256
     gu_tiles = [(f, min(gu_tile, ff_loc - f)) for f in range(0, ff_loc, gu_tile)]
@@ -225,8 +216,9 @@
                 buf[c, :, :, :, :, cs] = acc.astype(BF16).reshape(2, 2, 2, blk, half_d)
             for ab in range(2):
                 serve(base + ab)
-                down(cols[ab])
-                s0(1, c, ab)
+                down(pl.ds(ab * half_d, half_d))
+                start(1, c, 0, 2 * ab)
+                start(1, c, 0, 2 * ab + 1)
             return carry
         lax.fori_loop(0, n_chunks, chunk, 0)
 
@@ -234,13 +226,13 @@
     for j in range(n_k):
         for i in range(2):
             w_copy(i, j).start()
+    both(s1, 0, 0)
     p1(1)
-    both(s1, 0, 0)
     p1(2)
     for j in range(n_k):
         w_copy(2, j).start()
+    both(s2, 0, 0)
     both(s1, 0, 1)
-    both(s2, 0, 0)
     x_copy().wait()
     s3(0, 0)
     both(s2, 0, 1)
@@ -269,15 +261,15 @@
         (2, 5): [F(both, s2, 1, 1)],
         (2, 7): [F(both, g3, 1, 0)],
     })
+    both(s1, 1, 2)
     s3(1, 1)
+    both(s2, 1, 2)
+    both(g2, 1, 1)
+    s3(1, 2)
+    both(g3, 1, 1)
+    both(g2, 1, 2)
     fin(1, 0)
-    both(s1, 1, 2)
-    both(g2, 1, 1)
-    both(s2, 1, 2)
-    both(g3, 1, 1)
-    s3(1, 2)
     fin(1, 1)
-    both(g2, 1, 2)
     both(g3, 1, 2)
     fin(1, 2)
     for c in range(n_chunks):
@@ -310,8 +302,8 @@
             pltpu.VMEM((ff_loc, d_model), BF16),
             pltpu.VMEM((ff_loc, d_model), BF16),
             pltpu.VMEM((ff_loc, d_model), BF16),
-            pltpu.SemaphoreType.DMA((2, n_chunks, 12)),
-            pltpu.SemaphoreType.DMA((2, n_chunks, 12)),
+            pltpu.SemaphoreType.DMA((2, n_chunks, 24)),
+            pltpu.SemaphoreType.DMA((2, n_chunks, 24)),
             pltpu.SemaphoreType.DMA((3, 4)),
             pltpu.SemaphoreType.DMA((4,)),
             pltpu.SemaphoreType.DMA,
@@ -363,7 +355,7 @@
         sin_t[t] = jnp.sin(ang) * sign
 
     for j in range(n_k):
-        for cp in w_copies(j):
+        for cp in w_copies(j)[:2]:
             cp.wait()
     sq_lane = lax.broadcasted_iota(jnp.int32, (rows, rows), 1)
 
@@ -374,7 +366,7 @@
 
     def project(t):
         x_copy(t).wait()
-        res = jnp.dot(x[t], w[...], preferred_element_type=F32).astype(BF16)
+        res = jnp.dot(x[t], w[:, 0:q_loc + hd], preferred_element_type=F32).astype(BF16)
         raw[t] = res
         q = res[:, :q_loc].astype(F32)
         k = res[:, q_loc:q_loc + hd].astype(F32)
@@ -384,7 +376,6 @@
             pl.semaphore_wait(barrier, n_tp - 1)
         for d in range(n_tp - 1):
             send(t, d).start()
-        v_out[t] = res[:, q_loc + hd:width].astype(F32)
 
     def rotate_all(t):
         for d in range(n_tp - 1):
@@ -405,6 +396,10 @@
 
     for t in range(n_steps):
         project(t)
+    for j in range(n_k):
+        w_copies(j)[2].wait()
+    for t in range(n_steps):
+        v_out[t] = jnp.dot(x[t], w[:, q_loc + hd:width], preferred_element_type=F32).astype(BF16).astype(F32)
     q_out[pl.ds(n_steps * heads, rows, stride=16), :] = jnp.zeros((rows, hd), F32)
     for t in range(n_steps):
         rotate_all(t)
@@ -430,7 +425,7 @@
         scratch_shapes=[
             pltpu.VMEM((n_steps, rows, d_model), BF16),
             pltpu.VMEM((d_model, width), BF16),
-            pltpu.VMEM((n_steps, rows, width), BF16),
+            pltpu.VMEM((n_steps, rows, q_loc + hd), BF16),
             pltpu.VMEM((n_steps, rows, hd), F32),
             pltpu.VMEM((n_steps, rows, hd), F32),
             pltpu.VMEM((n_steps, n_tp, 8, rows), F32),

time: 135 us -> 130 us (0.963)
  Pallas kernels: 130 us -> 125 us
    pallas_call x1, Pallas kernels: 96.3 us -> 91.7 us  [tail(): pl.pallas_call(functools.partial(tail_kernel, dims), name='tail', out_sha...]
where the time goes in v5:
time: 130 us
  Pallas kernels  125 us (96%)
  local copies, waits for them, and re-layouts  4.29 us (3%)
    pallas_call x1, Pallas kernels, tail(): pl.pallas_call(functools.partial(tail_kernel, dims), name='tail', out_sha...  91.7 us
    pallas_call x1, Pallas kernels, head(): pl.pallas_call(functools.partial(head_kernel, (n_steps, rows, d_model, q_...  17.6 us
    pallas_call x1, Pallas kernels, attend(): pl.pallas_call(functools.partial(attn_kernel, (n_steps, nb, heads, hd, se...  15.4 us
    unnamed x1, local copies, waits for them, and re-layouts  4.29 us

profile of v5, /device:TPU:0, one launch (start us, length us, event | category | flops | bytes accessed | tf_op | source)
XLA Modules:
  0.0 129.6 jit_solution(2446766758831577152)
XLA Ops:
  0.6 17.6 %head.1 = (f32[2048,128]{1,0:T(8,128)}, f32[3,128,128]{2,1,0:T(8,128)}, f32[3,128,128]{2,1,0:T(8,128)}) custom-call(s32[1,128]{1,0:T(1,128)} %bitcast.28, bf16[5,128]{1,0:T(8,128)(2,1)} %bitcast.27, bf16[1,128]{1,0:T(2,128)(2,1)} %bitcast.29, f32[1,128]{1,0:T(1,128)} %constant.2.clone.freq_ref, bf16[3,128,5120]{2,1,0:T(8,128)(2,1)} %x_hbm.1, ...), custom_call_target="tpu_custom_call" | custom-call | tf_op jit(solution)/shard_map/head/pallas_call | solution.py:417
  18.3 15.4 %attend.1 = (bf16[3,128,640]{2,1,0:T(8,128)(2,1)}, bf16[128,256,128]{2,1,0:T(8,128)(2,1)}, bf16[128,256,128]{2,1,0:T(8,128)(2,1)}) custom-call(s32[128]{0:T(128)} %len_ref.1, f32[128,16,128]{2,1,0:T(8,128)} %bitcast.24, f32[3,128,128]{2,1,0:T(8,128)} %get-tuple-element.10.kn_ref, f32[3,128,128]{2,1,0:T(8,128)} %get-tuple-element.11.vn_ref, ...), custom_call_target="tpu_custom_call" | custom-call | flops 268435456 | bytes 33554432 | tf_op jit(solution)/shard_map/attend/pallas_call | solution.py:485
  33.6 91.7 %tail.1 = bf16[3,2,2,2,16,5120]{5,4,3,2,1,0:T(8,128)(2,1)} custom-call(bf16[3,128,640]{2,1,0:T(8,128)(2,1)} %get-tuple-element.12.o_ref, bf16[40,128]{1,0:T(8,128)(2,1)} %bitcast.25, bf16[40,128]{1,0:T(8,128)(2,1)} %bitcast.26, bf16[3,8,16,5120]{3,2,1,0:T(8,128)(2,1)} %bitcast.20, bf16[640,5120]{1,0:T(8,128)(2,1)} %wo_hbm.1, bf16[1728,5120]{1,0:T(8,128)(2,1)} %bitcast.18, ...), custom_call_target="tpu_custom_call" | custom-call | tf_op jit(solution)/shard_map/tail/pallas_call | solution.py:287
  125.3 4.3 %copy.22 = bf16[3,128,5120]{2,1,0:T(8,128)(2,1)} copy(bf16[3,128,5120]{2,1,0:T(8,128)(2,1)} %bitcast.21) | data formatting | bytes 7864320

commit v6 on v5

--- a/solution.py
+++ b/solution.py
@@ -438,64 +438,134 @@
     )(cache_len.reshape(1, -1), g_q.reshape(-1, hd), g_k.reshape(1, -1), freq, x_seq, w_q, w_k, w_v)
 
 
-def attn_kernel(dims, len_ref, q_ref, kn_ref, vn_ref, k_ref, v_ref, o_ref, ko_ref, vo_ref, s_scr, e_scr, l_scr, o_scr):
-    n_steps, nb, heads, hd, seq_max = dims
-    first = pl.program_id(0) * nb
+def attn_kernel(dims, len_ref, q_hbm, kn_hbm, vn_hbm, k_hbm, v_hbm, o_ref, ko_hbm, vo_hbm,
+                kb, vb, q, kn, vn, s_scr, e_scr, l_scr, o_scr, n_sem, in_sem, out_sem):
+    n_steps, nb, heads, hd, seq_max, n_rows = dims
+    n_blocks = n_rows // nb
     win = 32
     row_step = lax.broadcasted_iota(jnp.int32, (16, seq_max), 0) // heads
     col = lax.broadcasted_iota(jnp.int32, (16, seq_max), 1)
     ahead = col - row_step
     win_row = lax.broadcasted_iota(jnp.int32, (win, hd), 0)
-    for src, new, dst in ((k_ref, kn_ref, ko_ref), (v_ref, vn_ref, vo_ref)):
-        dst[...] = src[...]
+    small = [pltpu.make_async_copy(src, dst, n_sem.at[i])
+             for i, (src, dst) in enumerate(((kn_hbm, kn), (vn_hbm, vn), (q_hbm, q)))]
+
+    def load(i, blk):
+        src, dst = ((k_hbm, kb), (v_hbm, vb))[i]
+        rs = pl.ds(blk * nb, nb)
+        return pltpu.make_async_copy(src.at[rs], dst.at[rs], in_sem.at[i, blk])
+
+    def store(i, blk):
+        src, dst = ((kb, ko_hbm), (vb, vo_hbm))[i]
+        rs = pl.ds(blk * nb, nb)
+        return pltpu.make_async_copy(src.at[rs], dst.at[rs], out_sem.at[i, blk])
+
+    for i in range(2):
+        load(i, 0).start()
+    for cp in small:
+        cp.start()
+    for blk in range(1, n_blocks):
+        for i in range(2):
+            load(i, blk).start()
+    for cp in small:
+        cp.wait()
+
+    def block(blk, carry):
+        first = blk * nb
+        for j, (buf, new) in enumerate(((kb, kn), (vb, vn))):
+            load(j, blk).wait()
+            new_rows = [new[t, pl.ds(pl.multiple_of(first, nb), nb), :] for t in range(n_steps)]
+            for i in range(nb):
+                ln = len_ref[first + i]
+                base = pl.multiple_of(jnp.minimum((ln // 16) * 16, seq_max - win), 16)
+                rel = win_row + (base - ln)
+                cut = buf[first + i, pl.ds(base, win), :].astype(F32)
+                for t in range(n_steps):
+                    cut = jnp.where(rel == t, new_rows[t][i:i + 1, :], cut)
+                buf[first + i, pl.ds(base, win), :] = cut.astype(BF16)
+            store(j, blk).start()
         for i in range(nb):
-            ln = len_ref[first + i]
-            base = pl.multiple_of(jnp.minimum((ln // 16) * 16, seq_max - win), 16)
-            rel = win_row + (base - ln)
-            cut = src[i, pl.ds(base, win), :].astype(F32)
-            for t in range(n_steps):
-                cut = jnp.where(rel == t, new[t, i:i + 1, :], cut)
-            dst[i, pl.ds(base, win), :] = cut.astype(BF16)
-    for i in range(nb):
-        s = lax.dot_general(q_ref[i].astype(BF16), ko_ref[i], (((1,), (1,)), ((), ())), preferred_element_type=F32) * hd ** -0.5
-        s_scr[i * 16:(i + 1) * 16, :] = jnp.where(ahead <= len_ref[first + i], s, -jnp.inf)
-    for i in range(0, nb, 2):
-        rs = slice(i * 16, (i + 2) * 16)
-        s = s_scr[rs, :]
-        e = jnp.exp(s - jnp.max(s, axis=-1, keepdims=True))
-        l_scr[rs, :] = jnp.broadcast_to(jnp.sum(e, axis=-1, keepdims=True), (32, hd))
-        e_scr[rs, :] = e.astype(BF16)
-    for i in range(nb):
-        rs = slice(i * 16, (i + 1) * 16)
-        o_scr[rs, :] = jnp.dot(e_scr[rs, :], vo_ref[i], preferred_element_type=F32)
-    o_scr[...] = o_scr[...] / l_scr[...]
-    for t in range(n_steps):
-        for j in range(heads):
-            o_ref[t, :, j * hd:(j + 1) * hd] = o_scr[pl.ds(t * heads + j, nb, stride=16), :].astype(BF16)
+            s = lax.dot_general(q[first + i].astype(BF16), kb[first + i], (((1,), (1,)), ((), ())), preferred_element_type=F32) * hd ** -0.5
+            s_scr[i * 16:(i + 1) * 16, :] = jnp.where(ahead <= len_ref[first + i], s, -jnp.inf)
+        for i in range(0, nb, 2):
+            rs = slice(i * 16, (i + 2) * 16)
+            s = s_scr[rs, :]
+            e = jnp.exp(s - jnp.max(s, axis=-1, keepdims=True))
+            l_scr[rs, :] = jnp.broadcast_to(jnp.sum(e, axis=-1, keepdims=True), (32, hd))
+            e_scr[rs, :] = e.astype(BF16)
+        for i in range(nb):
+            rs = slice(i * 16, (i + 1) * 16)
+            o_scr[rs, :] = jnp.dot(e_scr[rs, :], vb[first + i], preferred_element_type=F32)
+        o_scr[...] = o_scr[...] / l_scr[...]
+        for t in range(n_steps):
+            for j in range(heads):
+                o_ref[t, pl.ds(pl.multiple_of(first, nb), nb), j * hd:(j + 1) * hd] = o_scr[pl.ds(t * heads + j, nb, stride=16), :].astype(BF16)
+        return carry
+    lax.fori_loop(0, n_blocks, block, 0)
+    for blk in range(n_blocks):
+        for i in range(2):
+            store(i, blk).wait()
 
 
 def attend(q, kn, vn, k_cache, v_cache, cache_len, heads):
     n_rows, _, seq_max, hd = k_cache.shape
     n_steps = kn.shape[0]
     nb = 32
-    cache_spec = pl.BlockSpec((nb, seq_max, hd), lambda i, ln: (i, 0, 0))
-    new_spec = pl.BlockSpec((n_steps, nb, hd), lambda i, ln: (0, i, 0))
+    hbm = pl.BlockSpec(memory_space=pl.ANY)
     cache_shape = jax.ShapeDtypeStruct((n_rows, seq_max, hd), BF16)
     flops = 4 * n_rows * 16 * seq_max * hd
     return pl.pallas_call(
-        functools.partial(attn_kernel, (n_steps, nb, heads, hd, seq_max)),
+        functools.partial(attn_kernel, (n_steps, nb, heads, hd, seq_max, n_rows)),
         name='attend',
-        grid_spec=pltpu.PrefetchScalarGridSpec(
-            num_scalar_prefetch=1,
-            grid=(n_rows // nb,),
-            in_specs=[pl.BlockSpec((nb, 16, hd), lambda i, ln: (i, 0, 0)), new_spec, new_spec, cache_spec, cache_spec],
-            out_specs=(pl.BlockSpec((n_steps, nb, heads * hd), lambda i, ln: (0, i, 0)), cache_spec, cache_spec),
-            scratch_shapes=[pltpu.VMEM((nb * 16, seq_max), F32), pltpu.VMEM((nb * 16, seq_max), BF16), pltpu.VMEM((nb * 16, hd), F32), pltpu.VMEM((nb * 16, hd), F32)],
-        ),
+        in_specs=[pl.BlockSpec(memory_space=pltpu.SMEM)] + [hbm] * 5,
+        out_specs=(pl.BlockSpec(memory_space=pltpu.VMEM), hbm, hbm),
+        scratch_shapes=[
+            pltpu.VMEM((n_rows, seq_max, hd), BF16),
+            pltpu.VMEM((n_rows, seq_max, hd), BF16),
+            pltpu.VMEM((n_rows, 16, hd), F32),
+            pltpu.VMEM((n_steps, n_rows, hd), F32),
+            pltpu.VMEM((n_steps, n_rows, hd), F32),
+            pltpu.VMEM((nb * 16, seq_max), F32),
+            pltpu.VMEM((nb * 16, seq_max), BF16),
+            pltpu.VMEM((nb * 16, hd), F32),
+            pltpu.VMEM((nb * 16, hd), F32),
+            pltpu.SemaphoreType.DMA((3,)),
+            pltpu.SemaphoreType.DMA((2, n_rows // nb)),
+            pltpu.SemaphoreType.DMA((2, n_rows // nb)),
+        ],
         out_shape=(jax.ShapeDtypeStruct((n_steps, n_rows, heads * hd), BF16), cache_shape, cache_shape),
         compiler_params=pltpu.CompilerParams(vmem_limit_bytes=67043328),
         cost_estimate=pl.CostEstimate(flops=flops, bytes_accessed=4 * n_rows * seq_max * hd * 2, transcendentals=n_rows * 16 * seq_max),
     )(cache_len, q.reshape(n_rows, 16, hd), kn, vn, k_cache[:, 0], v_cache[:, 0])
+
+
+def finish_kernel(n, src, dst, buf, in_sem, out_sem):
+    ins = [pltpu.make_async_copy(src.at[i], buf.at[i], in_sem.at[i]) for i in range(n)]
+    outs = [pltpu.make_async_copy(buf.at[i], dst.at[i], out_sem.at[i]) for i in range(n)]
+    for cp in ins:
+        cp.start()
+    for a, b in zip(ins, outs):
+        a.wait()
+        b.start()
+    for cp in outs:
+        cp.wait()
+
+
+def finish(y):
+    n_steps, rows, d_model = y.shape
+    n = 4 * n_steps
+    shape = (n, n_steps * rows // n, d_model)
+    hbm = pl.BlockSpec(memory_space=pl.ANY)
+    out = pl.pallas_call(
+        functools.partial(finish_kernel, n),
+        name='finish',
+        in_specs=[hbm],
+        out_specs=hbm,
+        scratch_shapes=[pltpu.VMEM(shape, BF16), pltpu.SemaphoreType.DMA((n,)), pltpu.SemaphoreType.DMA((n,))],
+        out_shape=jax.ShapeDtypeStruct(shape, BF16),
+        compiler_params=pltpu.CompilerParams(vmem_limit_bytes=67043328),
+    )(y.reshape(shape))
+    return out.reshape(y.shape)
 
 
 def local_layer(n_tp, x_seq, cache_len, k_cache, v_cache, w_q, w_k, w_v, w_o, w_gate, w_up, w_down, g_q, g_k, g_attn, g_mlp):
@@ -503,7 +573,7 @@
     q, kn, vn = head(x_seq, cache_len, w_q, w_k, w_v, g_q, g_k, n_tp)
     o, k_out, v_out = attend(q, kn, vn, k_cache, v_cache, cache_len, heads)
     y = tail(o, x_seq, w_o, w_gate, w_up, w_down, g_attn, g_mlp)
-    return y, k_out[:, None], v_out[:, None]
+    return finish(y), k_out[:, None], v_out[:, None]
 
 
 def solution(mesh):

time: 130 us -> 127 us (0.977)
  local copies, waits for them, and re-layouts: 4.29 us -> 0 us
    unnamed x1 -> x0, local copies, waits for them, and re-layouts: 4.29 us -> none
    pallas_call x0 -> x1, Pallas kernels: none -> 3.47 us  [finish(): pl.pallas_call(functools.partial(finish_kernel, n), name='finish', in_spe...]
    pallas_call x1, Pallas kernels: 15.4 us -> 13.3 us  [attend(): pl.pallas_call(functools.partial(attn_kernel, (n_steps, nb, heads, hd, se...]
where the time goes in v6:
time: 127 us
  Pallas kernels  126 us (99%)
    pallas_call x1, Pallas kernels, tail(): pl.pallas_call(functools.partial(tail_kernel, dims), name='tail', out_sha...  91.7 us
    pallas_call x1, Pallas kernels, head(): pl.pallas_call(functools.partial(head_kernel, (n_steps, rows, d_model, q_...  17.6 us
    pallas_call x1, Pallas kernels, attend(): pl.pallas_call(functools.partial(attn_kernel, (n_steps, nb, heads, hd, se...  13.3 us
    pallas_call x1, Pallas kernels, finish(): pl.pallas_call(functools.partial(finish_kernel, n), name='finish', in_spe...  3.47 us

profile of v6, /device:TPU:0, one launch (start us, length us, event | category | flops | bytes accessed | tf_op | source)
XLA Modules:
  0.0 126.9 jit_solution(2095735092746190446)
XLA Ops:
  0.6 17.6 %head.1 = (f32[2048,128]{1,0:T(8,128)}, f32[3,128,128]{2,1,0:T(8,128)}, f32[3,128,128]{2,1,0:T(8,128)}) custom-call(s32[1,128]{1,0:T(1,128)} %bitcast.30, bf16[5,128]{1,0:T(8,128)(2,1)} %bitcast.29, bf16[1,128]{1,0:T(2,128)(2,1)} %bitcast.31, f32[1,128]{1,0:T(1,128)} %constant.2.clone.freq_ref, bf16[3,128,5120]{2,1,0:T(8,128)(2,1)} %x_hbm.1, ...), custom_call_target="tpu_custom_call" | custom-call | tf_op jit(solution)/shard_map/head/pallas_call | solution.py:417
  18.3 13.3 %attend.1 = (bf16[3,128,640]{2,1,0:T(8,128)(2,1)}, bf16[128,256,128]{2,1,0:T(8,128)(2,1)}, bf16[128,256,128]{2,1,0:T(8,128)(2,1)}) custom-call(s32[128]{0:T(128)} %len_ref.1, f32[128,16,128]{2,1,0:T(8,128)} %bitcast.26, f32[3,128,128]{2,1,0:T(8,128)} %get-tuple-element.10.kn_hbm, f32[3,128,128]{2,1,0:T(8,128)} %get-tuple-element.11.vn_hbm, ...), custom_call_target="tpu_custom_call" | custom-call | flops 268435456 | bytes 33554432 | tf_op jit(solution)/shard_map/attend/pallas_call | solution.py:517
  31.6 91.7 %tail.1 = bf16[3,2,2,2,16,5120]{5,4,3,2,1,0:T(8,128)(2,1)} custom-call(bf16[3,128,640]{2,1,0:T(8,128)(2,1)} %get-tuple-element.12.o_ref, bf16[40,128]{1,0:T(8,128)(2,1)} %bitcast.27, bf16[40,128]{1,0:T(8,128)(2,1)} %bitcast.28, bf16[3,8,16,5120]{3,2,1,0:T(8,128)(2,1)} %bitcast.21, bf16[640,5120]{1,0:T(8,128)(2,1)} %wo_hbm.1, bf16[1728,5120]{1,0:T(8,128)(2,1)} %bitcast.19, ...), custom_call_target="tpu_custom_call" | custom-call | tf_op jit(solution)/shard_map/tail/pallas_call | solution.py:287
  123.3 3.5 %finish.1 = bf16[12,32,5120]{2,1,0:T(8,128)(2,1)} custom-call(bf16[12,32,5120]{2,1,0:T(8,128)(2,1)} %bitcast.22), custom_call_target="tpu_custom_call" | custom-call | tf_op jit(solution)/shard_map/finish/pallas_call | solution.py:559

commit v7 on v6

--- a/solution.py
+++ b/solution.py
@@ -167,12 +167,17 @@
             for p in range(n_p):
                 xfer(k, c, ph, p).wait_send()
 
-    def y_copy(c):
-        return pltpu.make_async_copy(buf.at[c], y_hbm.at[c], y_sem.at[c])
+    def y_copy(c, p):
+        cs = cols[p]
+        return pltpu.make_async_copy(buf.at[c, :, :, :, :, cs], y_hbm.at[c, :, :, :, :, cs], y_sem.at[c, p])
 
     def fin(k, c):
-        done(k, c)
-        y_copy(c).start()
+        for p in range(n_p):
+            xfer(k, c, 5, p).wait_recv()
+            y_copy(c, p).start()
+        for ph in range(3, 6):
+            for p in range(n_p):
+                xfer(k, c, ph, p).wait_send()
 
     def both(fn, k, c):
         for p in range(n_p):
@@ -273,7 +278,8 @@
     both(g3, 1, 2)
     fin(1, 2)
     for c in range(n_chunks):
-        y_copy(c).wait()
+        for p in range(n_p):
+            y_copy(c, p).wait()
 
 
 def tail(o, x_seq, w_o, w1, w3, w2, g_attn, g_mlp):
@@ -307,7 +313,7 @@
             pltpu.SemaphoreType.DMA((3, 4)),
             pltpu.SemaphoreType.DMA((4,)),
             pltpu.SemaphoreType.DMA,
-            pltpu.SemaphoreType.DMA((n_chunks,)),
+            pltpu.SemaphoreType.DMA((n_chunks, 4)),
             pltpu.SemaphoreType.REGULAR((2, n_chunks)),
         ],
         compiler_params=pltpu.CompilerParams(collective_id=1, has_side_effects=True, vmem_limit_bytes=67043328),
@@ -354,9 +360,6 @@
         cos_t[t] = jnp.cos(ang)
         sin_t[t] = jnp.sin(ang) * sign
 
-    for j in range(n_k):
-        for cp in w_copies(j)[:2]:
-            cp.wait()
     sq_lane = lax.broadcasted_iota(jnp.int32, (rows, rows), 1)
 
     def send(t, d):
@@ -366,7 +369,16 @@
 
     def project(t):
         x_copy(t).wait()
-        res = jnp.dot(x[t], w[:, 0:q_loc + hd], preferred_element_type=F32).astype(BF16)
+        if t == 0:
+            res = jnp.zeros((rows, q_loc + hd), F32)
+            for j in range(n_k):
+                for cp in w_copies(j)[:2]:
+                    cp.wait()
+                ks = slice(j * k_rows, (j + 1) * k_rows)
+                res = res + jnp.dot(x[t, :, ks], w[ks, 0:q_loc + hd], preferred_element_type=F32)
+            res = res.astype(BF16)
+        else:
+            res = jnp.dot(x[t], w[:, 0:q_loc + hd], preferred_element_type=F32).astype(BF16)
         raw[t] = res
         q = res[:, :q_loc].astype(F32)
         k = res[:, q_loc:q_loc + hd].astype(F32)
@@ -438,8 +450,8 @@
     )(cache_len.reshape(1, -1), g_q.reshape(-1, hd), g_k.reshape(1, -1), freq, x_seq, w_q, w_k, w_v)
 
 
-def attn_kernel(dims, len_ref, q_hbm, kn_hbm, vn_hbm, k_hbm, v_hbm, o_ref, ko_hbm, vo_hbm,
-                kb, vb, q, kn, vn, s_scr, e_scr, l_scr, o_scr, n_sem, in_sem, out_sem):
+def attn_kernel(dims, len_ref, q_hbm, kn_hbm, vn_hbm, k_hbm, v_hbm, o_hbm, ko_hbm, vo_hbm,
+                kb, vb, q, kn, vn, s_scr, e_scr, l_scr, o_scr, o_buf, n_sem, in_sem, out_sem, o_sem):
     n_steps, nb, heads, hd, seq_max, n_rows = dims
     n_blocks = n_rows // nb
     win = 32
@@ -460,20 +472,29 @@
         rs = pl.ds(blk * nb, nb)
         return pltpu.make_async_copy(src.at[rs], dst.at[rs], out_sem.at[i, blk])
 
-    for i in range(2):
-        load(i, 0).start()
-    for cp in small:
+    def o_store(blk):
+        rs = pl.ds(blk * nb, nb)
+        return pltpu.make_async_copy(o_buf.at[:, rs], o_hbm.at[:, rs], o_sem.at[blk])
+
+    small[0].start()
+    load(0, 0).start()
+    for cp in small[1:]:
         cp.start()
+    load(1, 0).start()
     for blk in range(1, n_blocks):
         for i in range(2):
             load(i, blk).start()
-    for cp in small:
-        cp.wait()
+    small[0].wait()
 
     def block(blk, carry):
         first = blk * nb
         for j, (buf, new) in enumerate(((kb, kn), (vb, vn))):
             load(j, blk).wait()
+            if j == 1:
+                @pl.when(blk == 0)
+                def _():
+                    for cp in small[1:]:
+                        cp.wait()
             new_rows = [new[t, pl.ds(pl.multiple_of(first, nb), nb), :] for t in range(n_steps)]
             for i in range(nb):
                 ln = len_ref[first + i]
@@ -499,12 +520,14 @@
         o_scr[...] = o_scr[...] / l_scr[...]
         for t in range(n_steps):
             for j in range(heads):
-                o_ref[t, pl.ds(pl.multiple_of(first, nb), nb), j * hd:(j + 1) * hd] = o_scr[pl.ds(t * heads + j, nb, stride=16), :].astype(BF16)
+                o_buf[t, pl.ds(pl.multiple_of(first, nb), nb), j * hd:(j + 1) * hd] = o_scr[pl.ds(t * heads + j, nb, stride=16), :].astype(BF16)
+        o_store(blk).start()
         return carry
     lax.fori_loop(0, n_blocks, block, 0)
     for blk in range(n_blocks):
         for i in range(2):
             store(i, blk).wait()
+        o_store(blk).wait()
 
 
 def attend(q, kn, vn, k_cache, v_cache, cache_len, heads):
@@ -518,7 +541,7 @@
         functools.partial(attn_kernel, (n_steps, nb, heads, hd, seq_max, n_rows)),
         name='attend',
         in_specs=[pl.BlockSpec(memory_space=pltpu.SMEM)] + [hbm] * 5,
-        out_specs=(pl.BlockSpec(memory_space=pltpu.VMEM), hbm, hbm),
+        out_specs=(hbm, hbm, hbm),
         scratch_shapes=[
             pltpu.VMEM((n_rows, seq_max, hd), BF16),
             pltpu.VMEM((n_rows, seq_max, hd), BF16),
@@ -529,9 +552,11 @@
             pltpu.VMEM((nb * 16, seq_max), BF16),
             pltpu.VMEM((nb * 16, hd), F32),
             pltpu.VMEM((nb * 16, hd), F32),
+            pltpu.VMEM((n_steps, n_rows, heads * hd), BF16),
             pltpu.SemaphoreType.DMA((3,)),
             pltpu.SemaphoreType.DMA((2, n_rows // nb)),
             pltpu.SemaphoreType.DMA((2, n_rows // nb)),
+            pltpu.SemaphoreType.DMA((n_rows // nb,)),
         ],
         out_shape=(jax.ShapeDtypeStruct((n_steps, n_rows, heads * hd), BF16), cache_shape, cache_shape),
         compiler_params=pltpu.CompilerParams(vmem_limit_bytes=67043328),

time: 127 us -> 126 us (level)
  no operation moved by 1% of the time
where the time goes in v7:
time: 126 us; the launch traced here: 125 us
  Pallas kernels  125 us (99%)
    pallas_call x1, Pallas kernels, tail(): pl.pallas_call(functools.partial(tail_kernel, dims), name='tail', out_sha...  90.8 us
    pallas_call x1, Pallas kernels, head(): pl.pallas_call(functools.partial(head_kernel, (n_steps, rows, d_model, q_...  17.2 us
    pallas_call x1, Pallas kernels, attend(): pl.pallas_call(functools.partial(attn_kernel, (n_steps, nb, heads, hd, se...  13.1 us
    pallas_call x1, Pallas kernels, finish(): pl.pallas_call(functools.partial(finish_kernel, n), name='finish', in_spe...  3.47 us

profile of v7, /device:TPU:0, one launch (start us, length us, event | category | flops | bytes accessed | tf_op | source)
XLA Modules:
  0.0 125.3 jit_solution(3861239025869028356)
XLA Ops:
  0.6 17.2 %head.1 = (f32[2048,128]{1,0:T(8,128)}, f32[3,128,128]{2,1,0:T(8,128)}, f32[3,128,128]{2,1,0:T(8,128)}) custom-call(s32[1,128]{1,0:T(1,128)} %bitcast.30, bf16[5,128]{1,0:T(8,128)(2,1)} %bitcast.29, bf16[1,128]{1,0:T(2,128)(2,1)} %bitcast.31, f32[1,128]{1,0:T(1,128)} %constant.2.clone.freq_ref, bf16[3,128,5120]{2,1,0:T(8,128)(2,1)} %x_hbm.1, ...), custom_call_target="tpu_custom_call" | custom-call | tf_op jit(solution)/shard_map/head/pallas_call | solution.py:429
  17.8 13.1 %attend.1 = (bf16[3,128,640]{2,1,0:T(8,128)(2,1)}, bf16[128,256,128]{2,1,0:T(8,128)(2,1)}, bf16[128,256,128]{2,1,0:T(8,128)(2,1)}) custom-call(s32[128]{0:T(128)} %len_ref.1, f32[128,16,128]{2,1,0:T(8,128)} %bitcast.26, f32[3,128,128]{2,1,0:T(8,128)} %get-tuple-element.10.kn_hbm, f32[3,128,128]{2,1,0:T(8,128)} %get-tuple-element.11.vn_hbm, ...), custom_call_target="tpu_custom_call" | custom-call | flops 268435456 | bytes 33554432 | tf_op jit(solution)/shard_map/attend/pallas_call | solution.py:540
  30.9 90.8 %tail.1 = bf16[3,2,2,2,16,5120]{5,4,3,2,1,0:T(8,128)(2,1)} custom-call(bf16[3,128,640]{2,1,0:T(8,128)(2,1)} %get-tuple-element.12.o_ref, bf16[40,128]{1,0:T(8,128)(2,1)} %bitcast.27, bf16[40,128]{1,0:T(8,128)(2,1)} %bitcast.28, bf16[3,8,16,5120]{3,2,1,0:T(8,128)(2,1)} %bitcast.21, bf16[640,5120]{1,0:T(8,128)(2,1)} %wo_hbm.1, bf16[1728,5120]{1,0:T(8,128)(2,1)} %bitcast.19, ...), custom_call_target="tpu_custom_call" | custom-call | tf_op jit(solution)/shard_map/tail/pallas_call | solution.py:293
  121.7 3.5 %finish.1 = bf16[12,32,5120]{2,1,0:T(8,128)(2,1)} custom-call(bf16[12,32,5120]{2,1,0:T(8,128)(2,1)} %bitcast.22), custom_call_target="tpu_custom_call" | custom-call | tf_op jit(solution)/shard_map/finish/pallas_call | solution.py:584

commit v8 on v7

--- a/solution.py
+++ b/solution.py
@@ -258,16 +258,16 @@
         (0, 6): [F(s3, 0, 2)],
         (1, 0): [F(done, 0, 1), F(both, g2, 0, 2)],
         (1, 1): [F(both, s1, 1, 0)],
-        (1, 4): [F(both, g3, 0, 2)],
         (1, 6): [F(both, s2, 1, 0)],
         (2, 0): [F(done, 0, 2), F(s3, 1, 0)],
         (2, 1): [F(both, s1, 1, 1)],
         (2, 3): [F(both, g2, 1, 0)],
         (2, 5): [F(both, s2, 1, 1)],
         (2, 7): [F(both, g3, 1, 0)],
+        (2, 8): [F(s3, 1, 1)],
+        (1, 5): [F(both, g3, 0, 2)],
     })
     both(s1, 1, 2)
-    s3(1, 1)
     both(s2, 1, 2)
     both(g2, 1, 1)
     s3(1, 2)

time: 126 us -> 124 us (0.984)
  Pallas kernels: 125 us -> 123 us
    pallas_call x1, Pallas kernels: 90.8 us -> 89 us  [tail(): pl.pallas_call(functools.partial(tail_kernel, dims), name='tail', out_sha...]
where the time goes in v8:
time: 124 us
  Pallas kernels  123 us (99%)
    pallas_call x1, Pallas kernels, tail(): pl.pallas_call(functools.partial(tail_kernel, dims), name='tail', out_sha...  89 us
    pallas_call x1, Pallas kernels, head(): pl.pallas_call(functools.partial(head_kernel, (n_steps, rows, d_model, q_...  17.2 us
    pallas_call x1, Pallas kernels, attend(): pl.pallas_call(functools.partial(attn_kernel, (n_steps, nb, heads, hd, se...  13.1 us
    pallas_call x1, Pallas kernels, finish(): pl.pallas_call(functools.partial(finish_kernel, n), name='finish', in_spe...  3.47 us

profile of v8, /device:TPU:0, one launch (start us, length us, event | category | flops | bytes accessed | tf_op | source)
XLA Modules:
  0.0 123.6 jit_solution(10049957519559303539)
XLA Ops:
  0.6 17.2 %head.1 = (f32[2048,128]{1,0:T(8,128)}, f32[3,128,128]{2,1,0:T(8,128)}, f32[3,128,128]{2,1,0:T(8,128)}) custom-call(s32[1,128]{1,0:T(1,128)} %bitcast.30, bf16[5,128]{1,0:T(8,128)(2,1)} %bitcast.29, bf16[1,128]{1,0:T(2,128)(2,1)} %bitcast.31, f32[1,128]{1,0:T(1,128)} %constant.2.clone.freq_ref, bf16[3,128,5120]{2,1,0:T(8,128)(2,1)} %x_hbm.1, ...), custom_call_target="tpu_custom_call" | custom-call | tf_op jit(solution)/shard_map/head/pallas_call | solution.py:429
  17.8 13.1 %attend.1 = (bf16[3,128,640]{2,1,0:T(8,128)(2,1)}, bf16[128,256,128]{2,1,0:T(8,128)(2,1)}, bf16[128,256,128]{2,1,0:T(8,128)(2,1)}) custom-call(s32[128]{0:T(128)} %len_ref.1, f32[128,16,128]{2,1,0:T(8,128)} %bitcast.26, f32[3,128,128]{2,1,0:T(8,128)} %get-tuple-element.10.kn_hbm, f32[3,128,128]{2,1,0:T(8,128)} %get-tuple-element.11.vn_hbm, ...), custom_call_target="tpu_custom_call" | custom-call | flops 268435456 | bytes 33554432 | tf_op jit(solution)/shard_map/attend/pallas_call | solution.py:540
  30.9 89.0 %tail.1 = bf16[3,2,2,2,16,5120]{5,4,3,2,1,0:T(8,128)(2,1)} custom-call(bf16[3,128,640]{2,1,0:T(8,128)(2,1)} %get-tuple-element.12.o_ref, bf16[40,128]{1,0:T(8,128)(2,1)} %bitcast.27, bf16[40,128]{1,0:T(8,128)(2,1)} %bitcast.28, bf16[3,8,16,5120]{3,2,1,0:T(8,128)(2,1)} %bitcast.21, bf16[640,5120]{1,0:T(8,128)(2,1)} %wo_hbm.1, bf16[1728,5120]{1,0:T(8,128)(2,1)} %bitcast.19, ...), custom_call_target="tpu_custom_call" | custom-call | tf_op jit(solution)/shard_map/tail/pallas_call | solution.py:293
  120.0 3.5 %finish.1 = bf16[12,32,5120]{2,1,0:T(8,128)(2,1)} custom-call(bf16[12,32,5120]{2,1,0:T(8,128)(2,1)} %bitcast.22), custom_call_target="tpu_custom_call" | custom-call | tf_op jit(solution)/shard_map/finish/pallas_call | solution.py:584
